TPU v7x, 32 devices: a whole 2x2x4 slice. The times are simulated.
32 devices in a mesh: row: 4 (over x, core), col: 8 (over z, y).
Axes of the slice: x: 2, y: 2, z: 4, core: 2. Of those that a mesh axis runs over, the one named last changes fastest.
Arguments:
- panel: bfloat16 [32768, 512], P('row', 'col'), may hold values from -0.03125 to 0.03125
- pheno: bfloat16 [32768, 2048], P('row', 'col'), may hold values from -48 to 48
- kin_values: float32 [512], replicated, may hold values from 0.1 to 10
- trait_values: float32 [128], replicated, may hold values from 0.1 to 10
- trait_basis: float32 [128, 128], replicated, may hold values from -0.5 to 0.5
Outputs:
- coeffs: float32 [512, 2048], P('row', 'col')
- genetic: bfloat16 [32768, 2048], P('row', 'col')
All inputs are finite; a program needn't handle non-finite values.
Results may differ from a plain program's by a relative error of at most 0.0049.
Values may be sent and summed in bfloat16 or wider, within the bound.
A program may use at most 64 MiB of HBM per device.

v0:
```python
import functools

import jax
import jax.numpy as jnp
from jax import lax
from jax.experimental import pallas as pl
from jax.experimental.pallas import tpu as pltpu
from jax.sharding import PartitionSpec as P

LANES = 128
PIECES = 4
MESH = pl.DeviceIdType.MESH
HIGH = lax.Precision.HIGHEST


def gather_rotate(
    rows, cols, q, pheno, basis_in, kin_in, trait_in,
    gen_out, coeffs_out,
    basis, kin, trait, w_out, c_out, held, gen_sem, g, ph, acc, part_f, part, rparts, sb, rb, ob, crow, ct,
    load_sem, send_sem, recv_sem, rs_send, rs_recv, a1_send, a1_recv, a2_send, a2_recv, ag_send, ag_recv,
):
    me_r, me_c = lax.axis_index("row"), lax.axis_index("col")
    lines = cols // 2
    z, y = me_c // 2, lax.rem(me_c, 2)
    other = me_c + 1 - 2 * y
    width, people = q.shape
    piece = people // PIECES
    columns = pheno.shape[1]
    traits = basis.shape[0]
    sets = columns * cols // traits
    t_here = traits // cols

    own_load = pltpu.make_async_copy(q, g.at[me_c], load_sem.at[0])
    own_load.start()
    ph_load = pltpu.make_async_copy(pheno, ph, load_sem.at[1])
    ph_load.start()
    small = [
        pltpu.make_async_copy(a, b, load_sem.at[2 + i])
        for i, (a, b) in enumerate(((basis_in, basis), (kin_in, kin), (trait_in, trait)))
    ]
    for copy in small:
        copy.start()

    barrier = pltpu.get_barrier_semaphore()
    for d in range(1, cols):
        pl.semaphore_signal(barrier, inc=1, device_id=(me_r, lax.rem(me_c + d, cols)), device_id_type=MESH)
    for d in range(1, rows):
        pl.semaphore_signal(barrier, inc=1, device_id=(lax.rem(me_r + d, rows), me_c), device_id_type=MESH)
    pl.semaphore_wait(barrier, cols + rows - 2)

    def hop(way, block, j):
        target = (jnp.minimum(me_c + 2, cols - 2 + y), jnp.maximum(me_c - 2, y), other)[way]
        here = g.at[block, :, pl.ds(j * piece, piece)]
        return pltpu.make_async_remote_copy(
            src_ref=here, dst_ref=here,
            send_sem=send_sem.at[way, block, j], recv_sem=recv_sem.at[block, j],
            device_id=(me_r, target), device_id_type=MESH,
        )

    def arrived(block, j):
        hop(2, block, j).wait_recv()

    up, down = z < lines - 1, z > 0
    late = PIECES // 2

    def line_sends(block, j, act):
        @pl.when(up)
        def _():
            act(hop(0, block, j))

        @pl.when(down)
        def _():
            act(hop(1, block, j))

    own_load.wait()
    for j in range(PIECES):
        line_sends(me_c, j, lambda h: h.start())
        hop(2, me_c, j).start()

    acc[...] = jnp.zeros_like(acc)
    ph_load.wait()

    def process(pair, j):
        arrived(2 * pair + 1 - y, j)
        lanes = pl.ds(pl.multiple_of(pair * LANES, LANES), LANES)
        at = pl.ds(j * piece, piece)
        lhs = jnp.concatenate([g[2 * pair, :, at], g[2 * pair + 1, :, at]], axis=0)
        acc[pair] += jnp.dot(lhs, ph[at, :], preferred_element_type=jnp.float32)
        w_out[at, lanes] = lhs.T

    def by_set(s):
        return part_f[pl.ds(s, t_here, stride=sets), :]

    def finish_pair(pair):
        @pl.when(pair != me_r)
        def _():
            part_f[...] = acc[pair].T
            for s in range(sets):
                part[pair, s * t_here:(s + 1) * t_here, :] = by_set(s).astype(jnp.bfloat16)
            reduce_copy(pair).start()

    def reduce_copy(pair):
        return pltpu.make_async_remote_copy(
            src_ref=part.at[pair], dst_ref=rparts.at[me_r],
            send_sem=rs_send.at[pair], recv_sem=rs_recv.at[me_r],
            device_id=(pair, me_c), device_id_type=MESH,
        )

    def around(s, fn):
        if s == 0:
            fn(z)
            return

        def side(i, _):
            pair = z - s + 2 * s * i

            @pl.when(jnp.logical_and(pair >= 0, pair < lines))
            def _():
                fn(pair)

            return 0

        lax.fori_loop(0, 2, side, 0)

    order = [(0, j) for j in range(PIECES)] + [(1, j) for j in range(late)]
    order += [(s, j) for s in range(2, lines) for j in range(PIECES)]
    tail = [(1, j) for j in range(late, PIECES)]
    done = 0

    def handle(s, j):
        around(s, lambda pair: process(pair, j))
        if j == PIECES - 1:
            around(s, finish_pair)

    for s in range(1, lines):
        for j in range(PIECES):
            skip = s == 1 and j >= late

            @pl.when(z - s >= 0)
            def _():
                b = me_c - 2 * s
                arrived(b, j)

                @pl.when(up)
                def _():
                    hop(0, b, j).start()

                if not skip:
                    hop(2, b, j).start()

            @pl.when(z + s < lines)
            def _():
                b = me_c + 2 * s
                arrived(b, j)

                @pl.when(down)
                def _():
                    hop(1, b, j).start()

                if not skip:
                    hop(2, b, j).start()

            if (s, j) != (1, 0):
                handle(*order[done])
                done += 1
    for j in range(late, PIECES):
        line_sends(other, j, lambda h: h.start())
    rest = order[done:]
    while rest or tail:
        if rest and len(rest) > len(tail):
            handle(*rest.pop(0))
        else:
            handle(*tail.pop(0))

    part_f[...] = acc[me_r].T
    total = jnp.concatenate([by_set(s) for s in range(sets)], axis=0)
    for d in range(1, rows):
        src = lax.rem(me_r + d, rows)
        pltpu.make_async_remote_copy(
            src_ref=part.at[src], dst_ref=rparts.at[src], send_sem=rs_send.at[src], recv_sem=rs_recv.at[src],
            device_id=(src, me_c), device_id_type=MESH,
        ).wait_recv()
        total = total + rparts[src].astype(jnp.float32)
    sb[...] = total.astype(jnp.bfloat16).reshape(sb.shape)

    def trade1(peer, slot):
        return pltpu.make_async_remote_copy(
            src_ref=sb.at[peer], dst_ref=rb.at[slot], send_sem=a1_send.at[peer], recv_sem=a1_recv.at[slot],
            device_id=(me_r, peer), device_id_type=MESH,
        )

    def trade2(peer, slot):
        return pltpu.make_async_remote_copy(
            src_ref=ob.at[peer], dst_ref=crow.at[me_r, slot], send_sem=a2_send.at[peer], recv_sem=a2_recv.at[slot],
            device_id=(me_r, peer), device_id_type=MESH,
        )

    def share(peer, slot):
        return pltpu.make_async_remote_copy(
            src_ref=crow.at[me_r], dst_ref=crow.at[slot], send_sem=ag_send.at[peer], recv_sem=ag_recv.at[slot],
            device_id=(peer, me_c), device_id_type=MESH,
        )

    col_peers = [lax.rem(me_c + d, cols) for d in range(1, cols)]
    row_peers = [lax.rem(me_r + d, rows) for d in range(1, rows)]
    for p in col_peers:
        trade1(p, me_c).start()
    rb[me_c] = sb[me_c]
    for copy in small:
        copy.wait()
    product = kin[pl.ds(me_r, 1), :] * jnp.broadcast_to(trait[...], (LANES, traits)).T
    weight = product / (product + 1.0)
    for p in col_peers:
        trade1(p, p).wait_recv()
    s_here = sets // cols
    got = jnp.concatenate(
        [rb[:, s * t_here:(s + 1) * t_here, :].astype(jnp.float32).reshape(traits, LANES) for s in range(s_here)], axis=1
    )
    rotated = jnp.dot(basis[...].T, got, precision=HIGH, preferred_element_type=jnp.float32)
    scaled = rotated * jnp.concatenate([weight] * s_here, axis=1)
    back = jnp.dot(basis[...], scaled, precision=HIGH, preferred_element_type=jnp.float32)
    for s in range(s_here):
        ob[:, s * t_here:(s + 1) * t_here, :] = (
            back[:, s * LANES:(s + 1) * LANES].reshape(cols, t_here, LANES).astype(jnp.bfloat16)
        )
    for p in col_peers:
        trade2(p, me_c).start()
    crow[me_r, me_c] = ob[me_c]
    for p in col_peers:
        trade2(p, p).wait_recv()
    for p in row_peers:
        share(p, me_r).start()

    def place(r):
        for s in range(sets):
            part_s = crow[r, s // s_here, (s % s_here) * t_here:(s % s_here + 1) * t_here, :]
            ct[pl.ds(s, t_here, stride=sets), :] = part_s.astype(jnp.float32)
        turned = ct[...].T
        c_out[pl.ds(pl.multiple_of(r * LANES, LANES), LANES), :] = turned.astype(jnp.bfloat16)
        return turned

    coeffs_out[...] = place(me_r)
    for p in row_peers:
        share(p, p).wait_recv()
        place(p)

    tiles = gen_sem.shape[0]
    size = people // tiles

    def emit(i):
        at = pl.ds(pl.multiple_of(i * size, size), size)
        return pltpu.make_async_copy(held.at[at], gen_out.at[at], gen_sem.at[i])

    def predict(i, _):
        at = pl.ds(pl.multiple_of(i * size, size), size)
        held[at, :] = jnp.dot(w_out[at, :], c_out[...], preferred_element_type=jnp.float32).astype(jnp.bfloat16)
        emit(i).start()
        return 0

    lax.fori_loop(0, tiles, predict, 0)

    for j in range(PIECES):
        line_sends(me_c, j, lambda h: h.wait_send())
        hop(2, me_c, j).wait_send()
        if j >= late:
            line_sends(other, j, lambda h: h.wait_send())
        for s in range(1, lines):
            skip = s == 1 and j >= late

            @pl.when(z - s >= 0)
            def _():
                @pl.when(up)
                def _():
                    hop(0, me_c - 2 * s, j).wait_send()

                if not skip:
                    hop(2, me_c - 2 * s, j).wait_send()

            @pl.when(z + s < lines)
            def _():
                @pl.when(down)
                def _():
                    hop(1, me_c + 2 * s, j).wait_send()

                if not skip:
                    hop(2, me_c + 2 * s, j).wait_send()

    for p in row_peers:
        reduce_copy(p).wait_send()
        share(p, me_r).wait_send()
    for p in col_peers:
        trade1(p, me_c).wait_send()
        trade2(p, me_c).wait_send()

    def finish(i, _):
        emit(i).wait()
        return 0

    lax.fori_loop(0, tiles, finish, 0)


def fused(panel, pheno, kin_values, trait_values, trait_basis):
    rows, cols = lax.axis_size("row"), lax.axis_size("col")
    ind, columns = pheno.shape
    traits = trait_basis.shape[0]
    sets = columns * cols // traits
    share = kin_values.shape[0] // rows
    bf, f32 = jnp.bfloat16, jnp.float32
    hbm = pl.BlockSpec(memory_space=pltpu.HBM)
    vmem = pl.BlockSpec(memory_space=pltpu.VMEM)
    lot = columns // cols
    dma = pltpu.SemaphoreType.DMA
    genetic, coeffs = pl.pallas_call(
        functools.partial(gather_rotate, rows, cols),
        out_shape=(
            jax.ShapeDtypeStruct((ind, columns), bf),
            jax.ShapeDtypeStruct((share, columns), f32),
        ),
        in_specs=[hbm] * 5,
        out_specs=(hbm, vmem),
        scratch_shapes=[
            pltpu.VMEM((traits, traits), f32),
            pltpu.VMEM((rows, share), f32),
            pltpu.VMEM((1, traits), f32),
            pltpu.VMEM((ind, rows * share), bf),
            pltpu.VMEM((rows * share, columns), bf),
            pltpu.VMEM((ind, columns), bf),
            dma((16,)),
            pltpu.VMEM((cols, panel.shape[1], ind), bf),
            pltpu.VMEM((ind, columns), bf),
            pltpu.VMEM((cols // 2, share, columns), f32),
            pltpu.VMEM((columns, LANES), f32),
            pltpu.VMEM((rows, columns, LANES), bf),
            pltpu.VMEM((rows, columns, LANES), bf),
            pltpu.VMEM((cols, lot, LANES), bf),
            pltpu.VMEM((cols, lot, LANES), bf),
            pltpu.VMEM((cols, lot, LANES), bf),
            pltpu.VMEM((rows, cols, lot, LANES), bf),
            pltpu.VMEM((columns, LANES), f32),
            dma((5,)), dma((3, cols, PIECES)), dma((cols, PIECES)),
            dma((rows,)), dma((rows,)), dma((cols,)), dma((cols,)), dma((cols,)), dma((cols,)),
            dma((rows,)), dma((rows,)),
        ],
        compiler_params=pltpu.CompilerParams(
            collective_id=0, has_side_effects=True, vmem_limit_bytes=56 * 1024 * 1024
        ),
    )(panel.T, pheno, trait_basis, kin_values.reshape(rows, share), trait_values[None, :])
    return coeffs, genetic


def local(panel, pheno, kin_values, trait_values, trait_basis):
    rows, cols = lax.axis_size("row"), lax.axis_size("col")
    eigen = kin_values.shape[0]
    if 2 * panel.shape[1] == LANES and eigen // rows == LANES and trait_basis.shape[0] // cols == 16:
        return fused(panel, pheno, kin_values, trait_values, trait_basis)
    return plain(panel, pheno, kin_values, trait_values, trait_basis)


def plain(panel, pheno, kin_values, trait_values, trait_basis):
    col_count = lax.axis_size("col")
    columns = pheno.shape[1]
    traits = trait_basis.shape[0]
    traits_here = traits // col_count
    set_count = columns // traits_here
    sets_dev = set_count // col_count
    whole_panel = lax.all_gather(panel, "col", axis=1, tiled=True)
    partial_value = lax.dot_general(
        whole_panel, pheno, (((0,), (0,)), ((), ())), preferred_element_type=jnp.float32
    )
    summed = lax.psum_scatter(partial_value, "row", scatter_dimension=0, tiled=True)
    first_row = lax.axis_index("row") * summed.shape[0]
    share_rows = summed.shape[0]
    by_trait = summed.reshape(share_rows, traits_here, set_count).transpose(0, 2, 1)
    by_trait = by_trait.reshape(share_rows, set_count * traits_here)
    grouped = lax.all_to_all(by_trait, "col", split_axis=1, concat_axis=1, tiled=True)
    grouped = grouped.reshape(share_rows, col_count, sets_dev, traits_here).transpose(0, 2, 1, 3)
    grouped = grouped.reshape(share_rows, sets_dev, traits)
    rotated = jnp.einsum("rst,tj->rsj", grouped, trait_basis, precision=HIGH)
    kin_rows = lax.dynamic_slice_in_dim(kin_values, first_row, share_rows, 0)
    product = kin_rows[:, None] * trait_values[None, :]
    scaled = rotated * (product / (product + 1.0))[:, None, :]
    unrotated = jnp.einsum("rsj,tj->rst", scaled, trait_basis, precision=HIGH)
    outgoing = unrotated.reshape(share_rows, sets_dev, col_count, traits_here).transpose(0, 2, 1, 3)
    outgoing = outgoing.reshape(share_rows, col_count * sets_dev * traits_here)
    returned = lax.all_to_all(outgoing, "col", split_axis=1, concat_axis=1, tiled=True)
    coeffs = returned.reshape(share_rows, set_count, traits_here).transpose(0, 2, 1)
    coeffs = coeffs.reshape(share_rows, columns)
    coeffs_low = lax.all_gather(coeffs.astype(jnp.bfloat16), "row", axis=0, tiled=True)
    genetic = jnp.dot(whole_panel, coeffs_low, preferred_element_type=jnp.float32)
    return (coeffs, genetic.astype(jnp.bfloat16))


def solution(mesh):
    return jax.shard_map(
        local,
        mesh=mesh,
        in_specs=(P("row", "col"), P("row", "col"), P(), P(), P()),
        out_specs=(P("row", "col"), P("row", "col")),
        check_vma=False,
    )
```

profile of v0, /device:TPU:0, one launch (start us, length us, event | category | flops | bytes accessed | tf_op | source)
XLA Modules:
  0.0 117.9 jit_solution(9972045244094061172)
XLA Ops:
  0.6 111.2 %shard_map.68 = (bf16[8192,256]{1,0:T(8,128)(2,1)}, f32[128,256]{1,0:T(8,128)}) custom-call(bf16[64,8192]{1,0:T(8,128)(2,1)} %bitcast.3, bf16[8192,256]{1,0:T(8,128)(2,1)} %pheno.1, f32[128,128]{1,0:T(8,128)} %basis_in.1, f32[4,128]{1,0:T(4,128)} %bitcast.4, f32[1,128]{1,0:T(1,128)} %bitcast.5), custom_call_target="tpu_custom_call" | custom-call | tf_op jit(solution)/shard_map/pallas_call | solution.py:313
  111.9 1.6 %copy.9 = f32[128,256]{1,0:T(8,128)} copy(f32[128,256]{1,0:T(8,128)} %get-tuple-element.8) | data formatting | bytes 262144
  113.4 4.5 %copy.10 = bf16[8192,256]{1,0:T(8,128)(2,1)} copy(bf16[8192,256]{1,0:T(8,128)(2,1)} %get-tuple-element.9) | data formatting | bytes 8388608
where the time goes:
time: 118 us
  Pallas kernels  111 us (94%)
  local copies, waits for them, and re-layouts  6.04 us (5%)
    pallas_call x1, Pallas kernels, fused(): pl.pallas_call(functools.partial(gather_rotate, rows, cols), out_shape=(j...  111 us
    unnamed x2, local copies, waits for them, and re-layouts  6.04 us

commit v1 on v0

--- a/solution.py
+++ b/solution.py
@@ -9,14 +9,15 @@
 
 LANES = 128
 PIECES = 4
+TILES = 16
 MESH = pl.DeviceIdType.MESH
 HIGH = lax.Precision.HIGHEST
 
 
 def gather_rotate(
     rows, cols, q, pheno, basis_in, kin_in, trait_in,
-    gen_out, coeffs_out,
-    basis, kin, trait, w_out, c_out, held, gen_sem, g, ph, acc, part_f, part, rparts, sb, rb, ob, crow, ct,
+    w_out, c_out,
+    basis, kin, trait, g, ph, acc, part_f, part, rparts, sb, rb, ob, crow, ct,
     load_sem, send_sem, recv_sem, rs_send, rs_recv, a1_send, a1_recv, a2_send, a2_recv, ag_send, ag_recv,
 ):
     me_r, me_c = lax.axis_index("row"), lax.axis_index("col")
@@ -235,29 +236,12 @@
         for s in range(sets):
             part_s = crow[r, s // s_here, (s % s_here) * t_here:(s % s_here + 1) * t_here, :]
             ct[pl.ds(s, t_here, stride=sets), :] = part_s.astype(jnp.float32)
-        turned = ct[...].T
-        c_out[pl.ds(pl.multiple_of(r * LANES, LANES), LANES), :] = turned.astype(jnp.bfloat16)
-        return turned
-
-    coeffs_out[...] = place(me_r)
+        c_out[pl.ds(pl.multiple_of(r * LANES, LANES), LANES), :] = ct[...].T.astype(jnp.bfloat16)
+
+    place(me_r)
     for p in row_peers:
         share(p, p).wait_recv()
         place(p)
-
-    tiles = gen_sem.shape[0]
-    size = people // tiles
-
-    def emit(i):
-        at = pl.ds(pl.multiple_of(i * size, size), size)
-        return pltpu.make_async_copy(held.at[at], gen_out.at[at], gen_sem.at[i])
-
-    def predict(i, _):
-        at = pl.ds(pl.multiple_of(i * size, size), size)
-        held[at, :] = jnp.dot(w_out[at, :], c_out[...], preferred_element_type=jnp.float32).astype(jnp.bfloat16)
-        emit(i).start()
-        return 0
-
-    lax.fori_loop(0, tiles, predict, 0)
 
     for j in range(PIECES):
         line_sends(me_c, j, lambda h: h.wait_send())
@@ -292,11 +276,30 @@
         trade1(p, me_c).wait_send()
         trade2(p, me_c).wait_send()
 
+
+def predict(w, c, gen_out, coeffs, held, gen_sem):
+    share = coeffs.shape[0]
+    size = w.shape[0] // TILES
+
+    def emit(i):
+        at = pl.ds(pl.multiple_of(i * size, size), size)
+        return pltpu.make_async_copy(held.at[at], gen_out.at[at], gen_sem.at[i])
+
+    def step(i, _):
+        at = pl.ds(pl.multiple_of(i * size, size), size)
+        held[at, :] = jnp.dot(w[at, :], c[...], preferred_element_type=jnp.float32).astype(jnp.bfloat16)
+        emit(i).start()
+        return 0
+
+    lax.fori_loop(0, TILES, step, 0)
+    mine = pl.ds(pl.multiple_of(lax.axis_index("row") * share, share), share)
+    coeffs[...] = c[mine, :].astype(jnp.float32)
+
     def finish(i, _):
         emit(i).wait()
         return 0
 
-    lax.fori_loop(0, tiles, finish, 0)
+    lax.fori_loop(0, TILES, finish, 0)
 
 
 def fused(panel, pheno, kin_values, trait_values, trait_basis):
@@ -310,22 +313,19 @@
     vmem = pl.BlockSpec(memory_space=pltpu.VMEM)
     lot = columns // cols
     dma = pltpu.SemaphoreType.DMA
-    genetic, coeffs = pl.pallas_call(
+    given = (panel.T, pheno, trait_basis, kin_values.reshape(rows, share), trait_values[None, :])
+    whole, low = pl.pallas_call(
         functools.partial(gather_rotate, rows, cols),
         out_shape=(
-            jax.ShapeDtypeStruct((ind, columns), bf),
-            jax.ShapeDtypeStruct((share, columns), f32),
+            pltpu.VMEM((ind, rows * share), bf),
+            pltpu.VMEM((rows * share, columns), bf),
         ),
         in_specs=[hbm] * 5,
-        out_specs=(hbm, vmem),
+        out_specs=(vmem, vmem),
         scratch_shapes=[
             pltpu.VMEM((traits, traits), f32),
             pltpu.VMEM((rows, share), f32),
             pltpu.VMEM((1, traits), f32),
-            pltpu.VMEM((ind, rows * share), bf),
-            pltpu.VMEM((rows * share, columns), bf),
-            pltpu.VMEM((ind, columns), bf),
-            dma((16,)),
             pltpu.VMEM((cols, panel.shape[1], ind), bf),
             pltpu.VMEM((ind, columns), bf),
             pltpu.VMEM((cols // 2, share, columns), f32),
@@ -342,9 +342,20 @@
             dma((rows,)), dma((rows,)),
         ],
         compiler_params=pltpu.CompilerParams(
-            collective_id=0, has_side_effects=True, vmem_limit_bytes=56 * 1024 * 1024
+            collective_id=0, has_side_effects=True, vmem_limit_bytes=30 * 1024 * 1024
         ),
-    )(panel.T, pheno, trait_basis, kin_values.reshape(rows, share), trait_values[None, :])
+    )(*(pltpu.with_memory_space_constraint(a, pltpu.HBM) for a in given))
+    genetic, coeffs = pl.pallas_call(
+        predict,
+        out_shape=(
+            jax.ShapeDtypeStruct((ind, columns), bf),
+            jax.ShapeDtypeStruct((share, columns), f32),
+        ),
+        in_specs=[vmem] * 2,
+        out_specs=(hbm, vmem),
+        scratch_shapes=[pltpu.VMEM((ind, columns), bf), dma((TILES,))],
+        compiler_params=pltpu.CompilerParams(vmem_limit_bytes=20 * 1024 * 1024),
+    )(whole, low)
     return coeffs, genetic
 
 

time: 118 us -> 112 us (0.949)
  local copies, waits for them, and re-layouts: 6.04 us -> 0 us
    unnamed x2 -> x0, local copies, waits for them, and re-layouts: 6.04 us -> none
    pallas_call x1 -> x2, Pallas kernels: 111 us -> 111 us  [the longest x1 105 us: fused(): pl.pallas_call(functools.partial(gather_rotate, rows, cols), out_shape=(p...]
where the time goes in v1:
time: 112 us
  Pallas kernels  111 us (99%)
    pallas_call x1, Pallas kernels, fused(): pl.pallas_call(functools.partial(gather_rotate, rows, cols), out_shape=(p...  105 us
    pallas_call x1, Pallas kernels, fused(): pl.pallas_call(predict, out_shape=(jax.ShapeDtypeStruct((ind, columns), b...  6.28 us

profile of v1, /device:TPU:0, one launch (start us, length us, event | category | flops | bytes accessed | tf_op | source)
XLA Modules:
  0.0 112.0 jit_solution(4334399510404207580)
XLA Ops:
  0.6 105.0 %shard_map.68 = (bf16[8192,512]{1,0:T(8,128)(2,1)S(1)}, bf16[512,256]{1,0:T(8,128)(2,1)S(1)}) custom-call(bf16[64,8192]{1,0:T(8,128)(2,1)} %bitcast.3, bf16[8192,256]{1,0:T(8,128)(2,1)} %pheno.1, f32[128,128]{1,0:T(8,128)} %basis_in.1, f32[4,128]{1,0:T(4,128)} %bitcast.4, f32[1,128]{1,0:T(1,128)} %bitcast.5), custom_call_target="tpu_custom_call" | custom-call | tf_op jit(solution)/shard_map/pallas_call | solution.py:317
  105.7 6.3 %shard_map.69 = (bf16[8192,256]{1,0:T(8,128)(2,1)}, f32[128,256]{1,0:T(8,128)}) custom-call(bf16[8192,512]{1,0:T(8,128)(2,1)S(1)} %get-tuple-element.6.w, bf16[512,256]{1,0:T(8,128)(2,1)S(1)} %get-tuple-element.7.c), custom_call_target="tpu_custom_call" | custom-call | tf_op jit(solution)/shard_map/pallas_call | solution.py:348

commit v2 on v1

--- a/solution.py
+++ b/solution.py
@@ -8,7 +8,11 @@
 from jax.sharding import PartitionSpec as P
 
 LANES = 128
-PIECES = 4
+PIECES = 8
+EARLY = (0, 1, 2, 3, 4, 5)
+LATE = (6, 7)
+FROM_END = (1, 2, 3, 4, 5)
+WAYS = (0, 1, 2, "y")
 TILES = 16
 MESH = pl.DeviceIdType.MESH
 HIGH = lax.Precision.HIGHEST
@@ -17,19 +21,21 @@
 def gather_rotate(
     rows, cols, q, pheno, basis_in, kin_in, trait_in,
     w_out, c_out,
-    basis, kin, trait, g, ph, acc, part_f, part, rparts, sb, rb, ob, crow, ct,
-    load_sem, send_sem, recv_sem, rs_send, rs_recv, a1_send, a1_recv, a2_send, a2_recv, ag_send, ag_recv,
+    basis, kin, trait, g, ph, lent, acc, lent_acc, part_f, part, rparts, sb, rb, ob, crow, ct,
+    load_sem, send_sem, recv_sem, lend_send, lend_recv,
+    rs_send, rs_recv, a1_send, a1_recv, a2_send, a2_recv, ag_send, ag_recv,
 ):
     me_r, me_c = lax.axis_index("row"), lax.axis_index("col")
     lines = cols // 2
     z, y = me_c // 2, lax.rem(me_c, 2)
-    other = me_c + 1 - 2 * y
     width, people = q.shape
     piece = people // PIECES
     columns = pheno.shape[1]
     traits = basis.shape[0]
     sets = columns * cols // traits
     t_here = traits // cols
+    late = people * len(LATE) // PIECES
+    lot = late // PIECES
 
     own_load = pltpu.make_async_copy(q, g.at[me_c], load_sem.at[0])
     own_load.start()
@@ -49,140 +55,248 @@
         pl.semaphore_signal(barrier, inc=1, device_id=(lax.rem(me_r + d, rows), me_c), device_id_type=MESH)
     pl.semaphore_wait(barrier, cols + rows - 2)
 
-    def hop(way, block, j):
-        target = (jnp.minimum(me_c + 2, cols - 2 + y), jnp.maximum(me_c - 2, y), other)[way]
+    far = z // (lines // 2)
+    place_of = lambda k: k + far * (lines - 1 - 2 * k)
+    is_end = z == place_of(0)
+    is_mid = jnp.logical_not(is_end)
+    own = lambda k: 2 * place_of(k) + y
+    across = lambda k: 2 * place_of(k) + 1 - y
+    SAME, OTHER = own, across
+
+    def hop(way, kind, k, j):
+        block = kind(k)
+        target = me_c + 1 - 2 * y if way == "y" else own(way)
         here = g.at[block, :, pl.ds(j * piece, piece)]
         return pltpu.make_async_remote_copy(
             src_ref=here, dst_ref=here,
-            send_sem=send_sem.at[way, block, j], recv_sem=recv_sem.at[block, j],
+            send_sem=send_sem.at[WAYS.index(way), block, j], recv_sem=recv_sem.at[block, j],
             device_id=(me_r, target), device_id_type=MESH,
         )
 
-    def arrived(block, j):
-        hop(2, block, j).wait_recv()
-
-    up, down = z < lines - 1, z > 0
-    late = PIECES // 2
-
-    def line_sends(block, j, act):
-        @pl.when(up)
-        def _():
-            act(hop(0, block, j))
-
-        @pl.when(down)
-        def _():
-            act(hop(1, block, j))
-
-    own_load.wait()
-    for j in range(PIECES):
-        line_sends(me_c, j, lambda h: h.start())
-        hop(2, me_c, j).start()
-
-    acc[...] = jnp.zeros_like(acc)
-    ph_load.wait()
-
-    def process(pair, j):
-        arrived(2 * pair + 1 - y, j)
-        lanes = pl.ds(pl.multiple_of(pair * LANES, LANES), LANES)
+    def lend(i):
+        return pltpu.make_async_remote_copy(
+            src_ref=pheno.at[pl.ds(people - late + i * lot, lot)], dst_ref=lent.at[pl.ds(i * lot, lot)],
+            send_sem=lend_send.at[i], recv_sem=lend_recv.at[i],
+            device_id=(me_r, own(1)), device_id_type=MESH,
+        )
+
+    def sender(role):
+        def send(way, kind, k, j):
+            role.append((way, kind, k, j))
+            hop(way, kind, k, j).start()
+
+        return send
+
+    def arrived(kind, k, j):
+        hop("y", kind, k, j).wait_recv()
+
+    def lhs_of(k, j):
+        pair = place_of(k)
         at = pl.ds(j * piece, piece)
-        lhs = jnp.concatenate([g[2 * pair, :, at], g[2 * pair + 1, :, at]], axis=0)
+        return pair, at, jnp.concatenate([g[2 * pair, :, at], g[2 * pair + 1, :, at]], axis=0)
+
+    def turn(pair, at, lhs):
+        w_out[at, pl.ds(pl.multiple_of(pair * LANES, LANES), LANES)] = lhs.T
+
+    def process(k, j):
+        pair, at, lhs = lhs_of(k, j)
         acc[pair] += jnp.dot(lhs, ph[at, :], preferred_element_type=jnp.float32)
-        w_out[at, lanes] = lhs.T
-
-    def by_set(s):
-        return part_f[pl.ds(s, t_here, stride=sets), :]
-
-    def finish_pair(pair):
+        turn(pair, at, lhs)
+
+    def process_lent(k, j):
+        pair, _, lhs = lhs_of(k, j)
+        theirs = lent[pl.ds((j - LATE[0]) * piece, piece), :]
+        lent_acc[pair] += jnp.dot(lhs, theirs, preferred_element_type=jnp.float32)
+
+    def reduce_copy(pair, h):
+        return pltpu.make_async_remote_copy(
+            src_ref=part.at[pair, h], dst_ref=rparts.at[me_r, h],
+            send_sem=rs_send.at[pair, h], recv_sem=rs_recv.at[me_r, h],
+            device_id=(pair, me_c), device_id_type=MESH,
+        )
+
+    def finish_pair(k, h=0):
+        pair = place_of(k)
+
         @pl.when(pair != me_r)
         def _():
-            part_f[...] = acc[pair].T
-            for s in range(sets):
-                part[pair, s * t_here:(s + 1) * t_here, :] = by_set(s).astype(jnp.bfloat16)
-            reduce_copy(pair).start()
-
-    def reduce_copy(pair):
-        return pltpu.make_async_remote_copy(
-            src_ref=part.at[pair], dst_ref=rparts.at[me_r],
-            send_sem=rs_send.at[pair], recv_sem=rs_recv.at[me_r],
-            device_id=(pair, me_c), device_id_type=MESH,
-        )
-
-    def around(s, fn):
-        if s == 0:
-            fn(z)
-            return
-
-        def side(i, _):
-            pair = z - s + 2 * s * i
-
-            @pl.when(jnp.logical_and(pair >= 0, pair < lines))
-            def _():
-                fn(pair)
-
-            return 0
-
-        lax.fori_loop(0, 2, side, 0)
-
-    order = [(0, j) for j in range(PIECES)] + [(1, j) for j in range(late)]
-    order += [(s, j) for s in range(2, lines) for j in range(PIECES)]
-    tail = [(1, j) for j in range(late, PIECES)]
-    done = 0
-
-    def handle(s, j):
-        around(s, lambda pair: process(pair, j))
-        if j == PIECES - 1:
-            around(s, finish_pair)
-
-    for s in range(1, lines):
+            part[pair, h] = (lent_acc if h else acc)[pair].astype(jnp.bfloat16)
+            reduce_copy(pair, h).start()
+
+    acc[...] = jnp.zeros_like(acc)
+    own_load.wait()
+    end_sent, mid_sent = [], []
+
+    @pl.when(is_end)
+    def _():
+        send = sender(end_sent)
         for j in range(PIECES):
-            skip = s == 1 and j >= late
-
-            @pl.when(z - s >= 0)
-            def _():
-                b = me_c - 2 * s
-                arrived(b, j)
-
-                @pl.when(up)
-                def _():
-                    hop(0, b, j).start()
-
-                if not skip:
-                    hop(2, b, j).start()
-
-            @pl.when(z + s < lines)
-            def _():
-                b = me_c + 2 * s
-                arrived(b, j)
-
-                @pl.when(down)
-                def _():
-                    hop(1, b, j).start()
-
-                if not skip:
-                    hop(2, b, j).start()
-
-            if (s, j) != (1, 0):
-                handle(*order[done])
-                done += 1
-    for j in range(late, PIECES):
-        line_sends(other, j, lambda h: h.start())
-    rest = order[done:]
-    while rest or tail:
-        if rest and len(rest) > len(tail):
-            handle(*rest.pop(0))
-        else:
-            handle(*tail.pop(0))
-
-    part_f[...] = acc[me_r].T
-    total = jnp.concatenate([by_set(s) for s in range(sets)], axis=0)
-    for d in range(1, rows):
-        src = lax.rem(me_r + d, rows)
-        pltpu.make_async_remote_copy(
-            src_ref=part.at[src], dst_ref=rparts.at[src], send_sem=rs_send.at[src], recv_sem=rs_recv.at[src],
-            device_id=(src, me_c), device_id_type=MESH,
-        ).wait_recv()
-        total = total + rparts[src].astype(jnp.float32)
-    sb[...] = total.astype(jnp.bfloat16).reshape(sb.shape)
+            send(1, SAME, 0, j)
+            if j in EARLY:
+                send("y", SAME, 0, j)
+        for i in range(PIECES):
+            lend(i).start()
+        ph_load.wait()
+        n = len(EARLY)
+        h = n // 2
+        for t in range(3 * n):
+            line, j = t // n, t % n
+            arrived(SAME, 1 + line, j)
+            if line or j < h:
+                send("y", SAME, 1 + line, j)
+            if line == 0:
+                arrived(OTHER, 0, j)
+                if j in FROM_END:
+                    send(1, OTHER, 0, j)
+                process(0, j)
+            elif t < n + h:
+                arrived(OTHER, 1, j)
+                process(1, j)
+            elif t < 2 * n + h:
+                arrived(OTHER, 2, t - n - h)
+                process(2, t - n - h)
+            else:
+                arrived(OTHER, 3, t - 2 * n - h)
+                process(3, t - 2 * n - h)
+            if t == n - 1:
+                finish_pair(0)
+            if t == 2 * n + h - 1:
+                finish_pair(2)
+        for j in range(h, n):
+            arrived(OTHER, 1, j)
+            process(1, j)
+            if j == n - 1:
+                finish_pair(1)
+            arrived(OTHER, 3, j)
+            process(3, j)
+        finish_pair(3)
+
+    @pl.when(is_mid)
+    def _():
+        send = sender(mid_sent)
+        n = len(EARLY)
+        for j in range(PIECES):
+            if j in EARLY:
+                send(0, SAME, 1, j)
+                send(2, SAME, 1, j)
+            send("y", SAME, 1, j)
+        lent_acc[...] = jnp.zeros_like(lent_acc)
+        ph_load.wait()
+        for j in range(PIECES):
+            arrived(SAME, 0, j)
+            if j in EARLY:
+                send(2, SAME, 0, j)
+            if j not in FROM_END:
+                send("y", SAME, 0, j)
+            if j in EARLY:
+                arrived(SAME, 2, j)
+                send(0, SAME, 2, j)
+                if j not in FROM_END:
+                    send("y", SAME, 2, j)
+            if j == n - 1:
+                for i in LATE:
+                    send(2, SAME, 1, i)
+            if j in LATE:
+                send(2, SAME, 0, j)
+                arrived(SAME, 3, j - n)
+                send(0, SAME, 3, j - n)
+                send("y", SAME, 3, j - n)
+            arrived(OTHER, 1, j)
+            process(1, j)
+        for j in FROM_END:
+            send(2, OTHER, 1, j)
+        finish_pair(1)
+        first = [j for j in range(PIECES) if j not in FROM_END]
+        b = len(LATE)
+        order = [(0, first[0]), (2, first[0])] + [(0, j) for j in first[1:]]
+        for i, (k, j) in enumerate(order):
+            lend(i).wait_recv()
+            arrived(SAME, 3, b + i)
+            send(0, SAME, 3, b + i)
+            send("y", SAME, 3, b + i)
+            arrived(OTHER, k, j)
+            process(k, j)
+        for j in EARLY[n // 2:]:
+            send(0, OTHER, 1, j)
+        for k in (0, 1):
+            process_lent(k, LATE[0])
+        done = len(order)
+        for i, (k, j) in enumerate([(2, j) for j in LATE] + [(3, j) for j in LATE]):
+            lend(done + i).wait_recv()
+            arrived(SAME, k, j)
+            send("y", SAME, k, j)
+            arrived(OTHER, 3, i)
+            process(3, i)
+        for k in (0, 1):
+            process_lent(k, LATE[1])
+            finish_pair(k, 1)
+        rest = [(3, j) for j in EARLY[2 * b:]] + [(2, j) for j in LATE] + [(3, j) for j in LATE]
+        for i, j in enumerate(FROM_END):
+            arrived(OTHER, 0, j)
+            process(0, j)
+            arrived(OTHER, 2, j)
+            process(2, j)
+            k, m = rest.pop(0)
+            arrived(OTHER, k, m)
+            process(k, m)
+            if m in LATE:
+                process_lent(k, m)
+        finish_pair(0)
+        finish_pair(2)
+        finish_pair(2, 1)
+        for k, m in rest:
+            arrived(OTHER, k, m)
+            process(k, m)
+            process_lent(k, m)
+        finish_pair(3)
+        finish_pair(3, 1)
+
+    end_bulk = [(None, SAME, 0, j) for j in LATE]
+    end_bulk += [("z", SAME, 1, LATE[0])]
+    end_bulk += [("z", SAME, k, j) for k in (2, 3) for j in LATE]
+    mid_bulk = [(SAME, k, j) for k in (1, 2, 3) for j in LATE] + [(OTHER, 1, LATE[1])]
+
+    def bulk(end_from, end_to, mid_from, mid_to):
+        @pl.when(is_end)
+        def _():
+            send = sender(end_sent)
+            for wait, kind, k, j in end_bulk[end_from:end_to]:
+                if wait:
+                    arrived(kind, k, j)
+                send("y", kind, k, j)
+
+        @pl.when(is_mid)
+        def _():
+            send = sender(mid_sent)
+            for kind, k, j in mid_bulk[mid_from:mid_to]:
+                send(0, kind, k, j)
+
+    bulk(0, 2, 0, 2)
+
+    def total_of(h):
+        total = (lent_acc if h else acc)[me_r]
+        for d in range(1, rows):
+            src = lax.rem(me_r + d, rows)
+            pltpu.make_async_remote_copy(
+                src_ref=part.at[src, h], dst_ref=rparts.at[src, h],
+                send_sem=rs_send.at[src, h], recv_sem=rs_recv.at[src, h],
+                device_id=(src, me_c), device_id_type=MESH,
+            ).wait_recv()
+            total = total + rparts[src, h].astype(jnp.float32)
+        part_f[...] = total.T
+        by_set = [part_f[pl.ds(s, t_here, stride=sets), :] for s in range(sets)]
+        turned = jnp.concatenate(by_set, axis=0).astype(jnp.bfloat16)
+        sb[:, h] = turned.reshape(cols, columns // cols, LANES)
+
+    total_of(0)
+
+    @pl.when(is_mid)
+    def _():
+        total_of(1)
+
+    @pl.when(is_end)
+    def _():
+        sb[:, 1] = jnp.zeros_like(sb[:, 1])
 
     def trade1(peer, slot):
         return pltpu.make_async_remote_copy(
@@ -206,6 +320,7 @@
     row_peers = [lax.rem(me_r + d, rows) for d in range(1, rows)]
     for p in col_peers:
         trade1(p, me_c).start()
+    bulk(2, 3, 2, 4)
     rb[me_c] = sb[me_c]
     for copy in small:
         copy.wait()
@@ -214,9 +329,18 @@
     for p in col_peers:
         trade1(p, p).wait_recv()
     s_here = sets // cols
-    got = jnp.concatenate(
-        [rb[:, s * t_here:(s + 1) * t_here, :].astype(jnp.float32).reshape(traits, LANES) for s in range(s_here)], axis=1
-    )
+
+    def gathered(s):
+        at = slice(s * t_here, (s + 1) * t_here)
+        terms = []
+        for c in range(cols):
+            term = rb[c, 0, at, :].astype(jnp.float32)
+            if c // 2 in (0, lines - 1):
+                term = term + rb[c + 2 if c // 2 == 0 else c - 2, 1, at, :].astype(jnp.float32)
+            terms.append(term)
+        return jnp.concatenate(terms, axis=0)
+
+    got = jnp.concatenate([gathered(s) for s in range(s_here)], axis=1)
     rotated = jnp.dot(basis[...].T, got, precision=HIGH, preferred_element_type=jnp.float32)
     scaled = rotated * jnp.concatenate([weight] * s_here, axis=1)
     back = jnp.dot(basis[...], scaled, precision=HIGH, preferred_element_type=jnp.float32)
@@ -226,11 +350,13 @@
         )
     for p in col_peers:
         trade2(p, me_c).start()
+    bulk(3, 5, 4, 6)
     crow[me_r, me_c] = ob[me_c]
     for p in col_peers:
         trade2(p, p).wait_recv()
     for p in row_peers:
         share(p, me_r).start()
+    bulk(5, 7, 6, 7)
 
     def place(r):
         for s in range(sets):
@@ -243,34 +369,32 @@
         share(p, p).wait_recv()
         place(p)
 
-    for j in range(PIECES):
-        line_sends(me_c, j, lambda h: h.wait_send())
-        hop(2, me_c, j).wait_send()
-        if j >= late:
-            line_sends(other, j, lambda h: h.wait_send())
-        for s in range(1, lines):
-            skip = s == 1 and j >= late
-
-            @pl.when(z - s >= 0)
-            def _():
-                @pl.when(up)
-                def _():
-                    hop(0, me_c - 2 * s, j).wait_send()
-
-                if not skip:
-                    hop(2, me_c - 2 * s, j).wait_send()
-
-            @pl.when(z + s < lines)
-            def _():
-                @pl.when(down)
-                def _():
-                    hop(1, me_c + 2 * s, j).wait_send()
-
-                if not skip:
-                    hop(2, me_c + 2 * s, j).wait_send()
+    def turn_late(k, j):
+        turn(*lhs_of(k, j))
+
+    @pl.when(is_end)
+    def _():
+        waited = [(kind, k, j) for wait, kind, k, j in end_bulk if wait]
+        for k in range(lines):
+            for j in LATE:
+                for kind in (SAME, OTHER):
+                    if (kind, k) != (SAME, 0) and (kind, k, j) not in waited:
+                        arrived(kind, k, j)
+                turn_late(k, j)
+        for way, kind, k, j in end_sent:
+            hop(way, kind, k, j).wait_send()
+        for i in range(PIECES):
+            lend(i).wait_send()
+
+    @pl.when(is_mid)
+    def _():
+        for way, kind, k, j in mid_sent:
+            hop(way, kind, k, j).wait_send()
+        for p in row_peers:
+            reduce_copy(p, 1).wait_send()
 
     for p in row_peers:
-        reduce_copy(p).wait_send()
+        reduce_copy(p, 0).wait_send()
         share(p, me_r).wait_send()
     for p in col_peers:
         trade1(p, me_c).wait_send()
@@ -328,21 +452,23 @@
             pltpu.VMEM((1, traits), f32),
             pltpu.VMEM((cols, panel.shape[1], ind), bf),
             pltpu.VMEM((ind, columns), bf),
-            pltpu.VMEM((cols // 2, share, columns), f32),
+            pltpu.VMEM((ind * len(LATE) // PIECES, columns), bf),
+            pltpu.VMEM((rows, share, columns), f32),
+            pltpu.VMEM((rows, share, columns), f32),
             pltpu.VMEM((columns, LANES), f32),
-            pltpu.VMEM((rows, columns, LANES), bf),
-            pltpu.VMEM((rows, columns, LANES), bf),
-            pltpu.VMEM((cols, lot, LANES), bf),
-            pltpu.VMEM((cols, lot, LANES), bf),
+            pltpu.VMEM((rows, 2, share, columns), bf),
+            pltpu.VMEM((rows, 2, share, columns), bf),
+            pltpu.VMEM((cols, 2, lot, LANES), bf),
+            pltpu.VMEM((cols, 2, lot, LANES), bf),
             pltpu.VMEM((cols, lot, LANES), bf),
             pltpu.VMEM((rows, cols, lot, LANES), bf),
             pltpu.VMEM((columns, LANES), f32),
-            dma((5,)), dma((3, cols, PIECES)), dma((cols, PIECES)),
-            dma((rows,)), dma((rows,)), dma((cols,)), dma((cols,)), dma((cols,)), dma((cols,)),
+            dma((5,)), dma((len(WAYS), cols, PIECES)), dma((cols, PIECES)), dma((PIECES,)), dma((PIECES,)),
+            dma((rows, 2)), dma((rows, 2)), dma((cols,)), dma((cols,)), dma((cols,)), dma((cols,)),
             dma((rows,)), dma((rows,)),
         ],
         compiler_params=pltpu.CompilerParams(
-            collective_id=0, has_side_effects=True, vmem_limit_bytes=30 * 1024 * 1024
+            collective_id=0, has_side_effects=True, vmem_limit_bytes=36 * 1024 * 1024
         ),
     )(*(pltpu.with_memory_space_constraint(a, pltpu.HBM) for a in given))
     genetic, coeffs = pl.pallas_call(
@@ -362,7 +488,8 @@
 def local(panel, pheno, kin_values, trait_values, trait_basis):
     rows, cols = lax.axis_size("row"), lax.axis_size("col")
     eigen = kin_values.shape[0]
-    if 2 * panel.shape[1] == LANES and eigen // rows == LANES and trait_basis.shape[0] // cols == 16:
+    fits = 2 * panel.shape[1] == LANES and eigen // rows == LANES and trait_basis.shape[0] // cols == 16
+    if fits and rows == 4 and cols == 2 * rows:
         return fused(panel, pheno, kin_values, trait_values, trait_basis)
     return plain(panel, pheno, kin_values, trait_values, trait_basis)
 

time: 112 us -> 106 us (0.946)
  Pallas kernels: 111 us -> 105 us
    pallas_call x1, Pallas kernels: 105 us -> 98.9 us  [fused(): pl.pallas_call(functools.partial(gather_rotate, rows, cols), out_shape=(p...]
where the time goes in v2:
time: 106 us
  Pallas kernels  105 us (99%)
    pallas_call x1, Pallas kernels, fused(): pl.pallas_call(functools.partial(gather_rotate, rows, cols), out_shape=(p...  98.9 us
    pallas_call x1, Pallas kernels, fused(): pl.pallas_call(predict, out_shape=(jax.ShapeDtypeStruct((ind, columns), b...  6.28 us

profile of v2, /device:TPU:0, one launch (start us, length us, event | category | flops | bytes accessed | tf_op | source)
XLA Modules:
  0.0 106.0 jit_solution(13118117061084226045)
XLA Ops:
  0.6 98.9 %shard_map.68 = (bf16[8192,512]{1,0:T(8,128)(2,1)S(1)}, bf16[512,256]{1,0:T(8,128)(2,1)S(1)}) custom-call(bf16[64,8192]{1,0:T(8,128)(2,1)} %bitcast.3, bf16[8192,256]{1,0:T(8,128)(2,1)} %pheno.1, f32[128,128]{1,0:T(8,128)} %basis_in.1, f32[4,128]{1,0:T(4,128)} %bitcast.4, f32[1,128]{1,0:T(1,128)} %bitcast.5), custom_call_target="tpu_custom_call" | custom-call | tf_op jit(solution)/shard_map/pallas_call | solution.py:441
  99.5 6.3 %shard_map.69 = (bf16[8192,256]{1,0:T(8,128)(2,1)}, f32[128,256]{1,0:T(8,128)}) custom-call(bf16[8192,512]{1,0:T(8,128)(2,1)S(1)} %get-tuple-element.6.w, bf16[512,256]{1,0:T(8,128)(2,1)S(1)} %get-tuple-element.7.c), custom_call_target="tpu_custom_call" | custom-call | tf_op jit(solution)/shard_map/pallas_call | solution.py:474

commit v3 on v2

--- a/solution.py
+++ b/solution.py
@@ -12,7 +12,24 @@
 EARLY = (0, 1, 2, 3, 4, 5)
 LATE = (6, 7)
 FROM_END = (1, 2, 3, 4, 5)
-WAYS = (0, 1, 2, "y")
+MID_FEED = 2
+UNITS = 4
+END_STEPS = (
+    ("P10", "P11"),
+    ("P20", "T00", "P21", "T01"),
+    ("P22", "T02"),
+    ("T03", "P23", "P30", "T10", "T11", "P31", "T20"),
+    ("P32", "P33", "T21", "T22", "T23"),
+    ("T30", "T31", "T32", "T33", "B12", "B13"),
+)
+MID_STEPS = (
+    ("O10", "O11", "O20", "O21", "O22"),
+    ("O23", "O30"),
+    ("O31", "O32"),
+    ("O33", "O12", "O13"),
+    ("X12", "X13"),
+    (),
+)
 TILES = 16
 MESH = pl.DeviceIdType.MESH
 HIGH = lax.Precision.HIGHEST
@@ -22,8 +39,7 @@
     rows, cols, q, pheno, basis_in, kin_in, trait_in,
     w_out, c_out,
     basis, kin, trait, g, ph, lent, acc, lent_acc, part_f, part, rparts, sb, rb, ob, crow, ct,
-    load_sem, send_sem, recv_sem, lend_send, lend_recv,
-    rs_send, rs_recv, a1_send, a1_recv, a2_send, a2_recv, ag_send, ag_recv,
+    load_sem, bulk_send, recv_sem, lend_recv, small_send, rs_recv, trade_recv, ag_recv,
 ):
     me_r, me_c = lax.axis_index("row"), lax.axis_index("col")
     lines = cols // 2
@@ -63,22 +79,35 @@
     across = lambda k: 2 * place_of(k) + 1 - y
     SAME, OTHER = own, across
 
+
+    def bank(way):
+        return 0 if way in (0, 1) else 1
+
+    def sends_done(counts):
+        for i, count in enumerate(counts):
+            rows_of = w_out.at[pl.ds(0, count * width * piece // w_out.shape[1])]
+            pltpu.make_async_copy(rows_of, rows_of, bulk_send.at[i]).wait()
+
     def hop(way, kind, k, j):
         block = kind(k)
         target = me_c + 1 - 2 * y if way == "y" else own(way)
         here = g.at[block, :, pl.ds(j * piece, piece)]
         return pltpu.make_async_remote_copy(
             src_ref=here, dst_ref=here,
-            send_sem=send_sem.at[WAYS.index(way), block, j], recv_sem=recv_sem.at[block, j],
+            send_sem=bulk_send.at[bank(way)], recv_sem=recv_sem.at[block, j],
             device_id=(me_r, target), device_id_type=MESH,
         )
 
     def lend(i):
         return pltpu.make_async_remote_copy(
             src_ref=pheno.at[pl.ds(people - late + i * lot, lot)], dst_ref=lent.at[pl.ds(i * lot, lot)],
-            send_sem=lend_send.at[i], recv_sem=lend_recv.at[i],
+            send_sem=bulk_send.at[0], recv_sem=lend_recv.at[i * len(LATE) // PIECES],
             device_id=(me_r, own(1)), device_id_type=MESH,
         )
+
+    def lent_here(i):
+        there = lent.at[pl.ds(i * piece, piece)]
+        pltpu.make_async_copy(there, there, lend_recv.at[i]).wait()
 
     def sender(role):
         def send(way, kind, k, j):
@@ -90,28 +119,27 @@
     def arrived(kind, k, j):
         hop("y", kind, k, j).wait_recv()
 
-    def lhs_of(k, j):
+    def lhs_of(k, at):
         pair = place_of(k)
-        at = pl.ds(j * piece, piece)
         return pair, at, jnp.concatenate([g[2 * pair, :, at], g[2 * pair + 1, :, at]], axis=0)
 
     def turn(pair, at, lhs):
         w_out[at, pl.ds(pl.multiple_of(pair * LANES, LANES), LANES)] = lhs.T
 
     def process(k, j):
-        pair, at, lhs = lhs_of(k, j)
+        pair, at, lhs = lhs_of(k, pl.ds(j * piece, piece))
         acc[pair] += jnp.dot(lhs, ph[at, :], preferred_element_type=jnp.float32)
         turn(pair, at, lhs)
 
     def process_lent(k, j):
-        pair, _, lhs = lhs_of(k, j)
+        pair, _, lhs = lhs_of(k, pl.ds(j * piece, piece))
         theirs = lent[pl.ds((j - LATE[0]) * piece, piece), :]
         lent_acc[pair] += jnp.dot(lhs, theirs, preferred_element_type=jnp.float32)
 
     def reduce_copy(pair, h):
         return pltpu.make_async_remote_copy(
-            src_ref=part.at[pair, h], dst_ref=rparts.at[me_r, h],
-            send_sem=rs_send.at[pair, h], recv_sem=rs_recv.at[me_r, h],
+            src_ref=part.at[h, pair], dst_ref=rparts.at[h, me_r],
+            send_sem=small_send.at[h], recv_sem=rs_recv.at[h],
             device_id=(pair, me_c), device_id_type=MESH,
         )
 
@@ -120,8 +148,40 @@
 
         @pl.when(pair != me_r)
         def _():
-            part[pair, h] = (lent_acc if h else acc)[pair].astype(jnp.bfloat16)
+            part[h, pair] = (lent_acc if h else acc)[pair].astype(jnp.bfloat16)
             reduce_copy(pair, h).start()
+
+    def unit(u):
+        size = late // UNITS
+        return pl.ds(people - late + u * size, size)
+
+    def late_hop(way, kind, k, u):
+        block = kind(k)
+        here = g.at[block, :, unit(u)]
+        return pltpu.make_async_remote_copy(
+            src_ref=here, dst_ref=here, send_sem=bulk_send.at[0], recv_sem=recv_sem.at[block, len(EARLY) + u],
+            device_id=(me_r, me_c + 1 - 2 * y if way == "y" else own(way)), device_id_type=MESH,
+        )
+
+    late_sent = {"end": [], "mid": []}
+
+    def late_send_off(role, way, kind, k, u):
+        late_sent[role].append((way, kind, k, u))
+        late_hop(way, kind, k, u).start()
+
+    def late_steps(role, i):
+        for what, k, u in (END_STEPS if role == "end" else MID_STEPS)[i]:
+            k, u = int(k), int(u)
+            if what == "P":
+                late_hop("y", SAME, k, u).wait_recv()
+                late_send_off(role, "y", SAME, k, u)
+            elif what in "OX":
+                late_send_off(role, 0, SAME if what == "O" else OTHER, k, u)
+            else:
+                if what == "B":
+                    late_hop("y", SAME, k, u).wait_recv()
+                late_hop("y", OTHER, k, u).wait_recv()
+                turn(*lhs_of(k, unit(u)))
 
     acc[...] = jnp.zeros_like(acc)
     own_load.wait()
@@ -162,6 +222,8 @@
                 finish_pair(0)
             if t == 2 * n + h - 1:
                 finish_pair(2)
+        for u in range(UNITS):
+            late_send_off("end", "y", SAME, 0, u)
         for j in range(h, n):
             arrived(OTHER, 1, j)
             process(1, j)
@@ -170,6 +232,7 @@
             arrived(OTHER, 3, j)
             process(3, j)
         finish_pair(3)
+        late_steps("end", 0)
 
     @pl.when(is_mid)
     def _():
@@ -210,7 +273,6 @@
         b = len(LATE)
         order = [(0, first[0]), (2, first[0])] + [(0, j) for j in first[1:]]
         for i, (k, j) in enumerate(order):
-            lend(i).wait_recv()
             arrived(SAME, 3, b + i)
             send(0, SAME, 3, b + i)
             send("y", SAME, 3, b + i)
@@ -218,15 +280,15 @@
             process(k, j)
         for j in EARLY[n // 2:]:
             send(0, OTHER, 1, j)
+        lent_here(0)
         for k in (0, 1):
             process_lent(k, LATE[0])
-        done = len(order)
         for i, (k, j) in enumerate([(2, j) for j in LATE] + [(3, j) for j in LATE]):
-            lend(done + i).wait_recv()
             arrived(SAME, k, j)
             send("y", SAME, k, j)
             arrived(OTHER, 3, i)
             process(3, i)
+        lent_here(1)
         for k in (0, 1):
             process_lent(k, LATE[1])
             finish_pair(k, 1)
@@ -241,6 +303,8 @@
             process(k, m)
             if m in LATE:
                 process_lent(k, m)
+            if i == MID_FEED:
+                late_steps("mid", 0)
         finish_pair(0)
         finish_pair(2)
         finish_pair(2, 1)
@@ -251,38 +315,24 @@
         finish_pair(3)
         finish_pair(3, 1)
 
-    end_bulk = [(None, SAME, 0, j) for j in LATE]
-    end_bulk += [("z", SAME, 1, LATE[0])]
-    end_bulk += [("z", SAME, k, j) for k in (2, 3) for j in LATE]
-    mid_bulk = [(SAME, k, j) for k in (1, 2, 3) for j in LATE] + [(OTHER, 1, LATE[1])]
-
-    def bulk(end_from, end_to, mid_from, mid_to):
+    def exchange_time(i):
         @pl.when(is_end)
         def _():
-            send = sender(end_sent)
-            for wait, kind, k, j in end_bulk[end_from:end_to]:
-                if wait:
-                    arrived(kind, k, j)
-                send("y", kind, k, j)
+            late_steps("end", i)
 
         @pl.when(is_mid)
         def _():
-            send = sender(mid_sent)
-            for kind, k, j in mid_bulk[mid_from:mid_to]:
-                send(0, kind, k, j)
-
-    bulk(0, 2, 0, 2)
+            late_steps("mid", i)
+
+    def all_but_one(ref, sem):
+        some = ref.at[pl.ds(0, ref.shape[0] - 1)]
+        pltpu.make_async_copy(some, some, sem).wait()
 
     def total_of(h):
+        all_but_one(rparts.at[h], rs_recv.at[h])
         total = (lent_acc if h else acc)[me_r]
         for d in range(1, rows):
-            src = lax.rem(me_r + d, rows)
-            pltpu.make_async_remote_copy(
-                src_ref=part.at[src, h], dst_ref=rparts.at[src, h],
-                send_sem=rs_send.at[src, h], recv_sem=rs_recv.at[src, h],
-                device_id=(src, me_c), device_id_type=MESH,
-            ).wait_recv()
-            total = total + rparts[src, h].astype(jnp.float32)
+            total = total + rparts[h, lax.rem(me_r + d, rows)].astype(jnp.float32)
         part_f[...] = total.T
         by_set = [part_f[pl.ds(s, t_here, stride=sets), :] for s in range(sets)]
         turned = jnp.concatenate(by_set, axis=0).astype(jnp.bfloat16)
@@ -300,19 +350,19 @@
 
     def trade1(peer, slot):
         return pltpu.make_async_remote_copy(
-            src_ref=sb.at[peer], dst_ref=rb.at[slot], send_sem=a1_send.at[peer], recv_sem=a1_recv.at[slot],
+            src_ref=sb.at[peer], dst_ref=rb.at[slot], send_sem=small_send.at[2], recv_sem=trade_recv.at[0],
             device_id=(me_r, peer), device_id_type=MESH,
         )
 
     def trade2(peer, slot):
         return pltpu.make_async_remote_copy(
-            src_ref=ob.at[peer], dst_ref=crow.at[me_r, slot], send_sem=a2_send.at[peer], recv_sem=a2_recv.at[slot],
+            src_ref=ob.at[peer], dst_ref=crow.at[me_r, slot], send_sem=small_send.at[3], recv_sem=trade_recv.at[1],
             device_id=(me_r, peer), device_id_type=MESH,
         )
 
     def share(peer, slot):
         return pltpu.make_async_remote_copy(
-            src_ref=crow.at[me_r], dst_ref=crow.at[slot], send_sem=ag_send.at[peer], recv_sem=ag_recv.at[slot],
+            src_ref=crow.at[me_r], dst_ref=crow.at[slot], send_sem=small_send.at[4], recv_sem=ag_recv.at[slot],
             device_id=(peer, me_c), device_id_type=MESH,
         )
 
@@ -320,14 +370,14 @@
     row_peers = [lax.rem(me_r + d, rows) for d in range(1, rows)]
     for p in col_peers:
         trade1(p, me_c).start()
-    bulk(2, 3, 2, 4)
+    exchange_time(1)
+    exchange_time(2)
     rb[me_c] = sb[me_c]
     for copy in small:
         copy.wait()
     product = kin[pl.ds(me_r, 1), :] * jnp.broadcast_to(trait[...], (LANES, traits)).T
     weight = product / (product + 1.0)
-    for p in col_peers:
-        trade1(p, p).wait_recv()
+    all_but_one(rb, trade_recv.at[0])
     s_here = sets // cols
 
     def gathered(s):
@@ -350,13 +400,11 @@
         )
     for p in col_peers:
         trade2(p, me_c).start()
-    bulk(3, 5, 4, 6)
+    exchange_time(3)
     crow[me_r, me_c] = ob[me_c]
-    for p in col_peers:
-        trade2(p, p).wait_recv()
+    all_but_one(ob, trade_recv.at[1])
     for p in row_peers:
         share(p, me_r).start()
-    bulk(5, 7, 6, 7)
 
     def place(r):
         for s in range(sets):
@@ -365,65 +413,49 @@
         c_out[pl.ds(pl.multiple_of(r * LANES, LANES), LANES), :] = ct[...].T.astype(jnp.bfloat16)
 
     place(me_r)
+    exchange_time(4)
     for p in row_peers:
         share(p, p).wait_recv()
         place(p)
-
-    def turn_late(k, j):
-        turn(*lhs_of(k, j))
+    exchange_time(5)
+
+    def count(sent, others, late):
+        counts = [others + late * piece_of_unit, 0]
+        for way, *_ in sent:
+            counts[bank(way)] += 1
+        return counts
+
+    piece_of_unit = late / (UNITS * piece)
 
     @pl.when(is_end)
     def _():
-        waited = [(kind, k, j) for wait, kind, k, j in end_bulk if wait]
-        for k in range(lines):
-            for j in LATE:
-                for kind in (SAME, OTHER):
-                    if (kind, k) != (SAME, 0) and (kind, k, j) not in waited:
-                        arrived(kind, k, j)
-                turn_late(k, j)
-        for way, kind, k, j in end_sent:
-            hop(way, kind, k, j).wait_send()
-        for i in range(PIECES):
-            lend(i).wait_send()
+        sends_done([int(c) for c in count(end_sent, PIECES, len(late_sent["end"]))])
 
     @pl.when(is_mid)
     def _():
-        for way, kind, k, j in mid_sent:
-            hop(way, kind, k, j).wait_send()
-        for p in row_peers:
-            reduce_copy(p, 1).wait_send()
-
-    for p in row_peers:
-        reduce_copy(p, 0).wait_send()
-        share(p, me_r).wait_send()
-    for p in col_peers:
-        trade1(p, me_c).wait_send()
-        trade2(p, me_c).wait_send()
-
-
-def predict(w, c, gen_out, coeffs, held, gen_sem):
+        sends_done([int(c) for c in count(mid_sent, 0, len(late_sent["mid"]))])
+        all_but_one(part.at[1], small_send.at[1])
+
+    all_but_one(part.at[0], small_send.at[0])
+    all_but_one(sb, small_send.at[2])
+    all_but_one(ob, small_send.at[3])
+    all_but_one(crow, small_send.at[4])
+
+
+def predict(w, c, gen_out, coeffs_out, held, coeffs, gen_sem):
     share = coeffs.shape[0]
     size = w.shape[0] // TILES
-
-    def emit(i):
-        at = pl.ds(pl.multiple_of(i * size, size), size)
-        return pltpu.make_async_copy(held.at[at], gen_out.at[at], gen_sem.at[i])
-
-    def step(i, _):
-        at = pl.ds(pl.multiple_of(i * size, size), size)
-        held[at, :] = jnp.dot(w[at, :], c[...], preferred_element_type=jnp.float32).astype(jnp.bfloat16)
-        emit(i).start()
-        return 0
-
-    lax.fori_loop(0, TILES, step, 0)
     mine = pl.ds(pl.multiple_of(lax.axis_index("row") * share, share), share)
     coeffs[...] = c[mine, :].astype(jnp.float32)
-
-    def finish(i, _):
-        emit(i).wait()
-        return 0
-
-    lax.fori_loop(0, TILES, finish, 0)
+    copies = [pltpu.make_async_copy(coeffs, coeffs_out, gen_sem.at[TILES])]
+    copies[0].start()
+    for i in range(TILES):
+        at = pl.ds(i * size, size)
+        held[at, :] = jnp.dot(w[at, :], c[...], preferred_element_type=jnp.float32).astype(jnp.bfloat16)
+        copies.append(pltpu.make_async_copy(held.at[at], gen_out.at[at], gen_sem.at[i]))
+        copies[-1].start()
+    for copy in copies:
+        copy.wait()
 
 
 def fused(panel, pheno, kin_values, trait_values, trait_basis):
@@ -456,16 +488,14 @@
             pltpu.VMEM((rows, share, columns), f32),
             pltpu.VMEM((rows, share, columns), f32),
             pltpu.VMEM((columns, LANES), f32),
-            pltpu.VMEM((rows, 2, share, columns), bf),
-            pltpu.VMEM((rows, 2, share, columns), bf),
+            pltpu.VMEM((2, rows, share, columns), bf),
+            pltpu.VMEM((2, rows, share, columns), bf),
             pltpu.VMEM((cols, 2, lot, LANES), bf),
             pltpu.VMEM((cols, 2, lot, LANES), bf),
             pltpu.VMEM((cols, lot, LANES), bf),
             pltpu.VMEM((rows, cols, lot, LANES), bf),
             pltpu.VMEM((columns, LANES), f32),
-            dma((5,)), dma((len(WAYS), cols, PIECES)), dma((cols, PIECES)), dma((PIECES,)), dma((PIECES,)),
-            dma((rows, 2)), dma((rows, 2)), dma((cols,)), dma((cols,)), dma((cols,)), dma((cols,)),
-            dma((rows,)), dma((rows,)),
+            dma((5,)), dma((2,)), dma((cols, len(EARLY) + UNITS)), dma((len(LATE),)), dma((5,)), dma((2,)), dma((2,)), dma((rows,)),
         ],
         compiler_params=pltpu.CompilerParams(
             collective_id=0, has_side_effects=True, vmem_limit_bytes=36 * 1024 * 1024
@@ -478,8 +508,8 @@
             jax.ShapeDtypeStruct((share, columns), f32),
         ),
         in_specs=[vmem] * 2,
-        out_specs=(hbm, vmem),
-        scratch_shapes=[pltpu.VMEM((ind, columns), bf), dma((TILES,))],
+        out_specs=(hbm, hbm),
+        scratch_shapes=[pltpu.VMEM((ind, columns), bf), pltpu.VMEM((share, columns), f32), dma((TILES + 1,))],
         compiler_params=pltpu.CompilerParams(vmem_limit_bytes=20 * 1024 * 1024),
     )(whole, low)
     return coeffs, genetic

time: 106 us -> 94.3 us (0.89)
  Pallas kernels: 105 us -> 93.4 us
    pallas_call x1, Pallas kernels: 98.9 us -> 89.9 us  [fused(): pl.pallas_call(functools.partial(gather_rotate, rows, cols), out_shape=(p...]
    pallas_call x1, Pallas kernels: 6.28 us -> 3.44 us  [fused(): pl.pallas_call(predict, out_shape=(jax.ShapeDtypeStruct((ind, columns), b...]
where the time goes in v3:
time: 94.3 us; the launch traced here: 94.2 us
  Pallas kernels  93.4 us (99%)
    pallas_call x1, Pallas kernels, fused(): pl.pallas_call(functools.partial(gather_rotate, rows, cols), out_shape=(p...  89.9 us
    pallas_call x1, Pallas kernels, fused(): pl.pallas_call(predict, out_shape=(jax.ShapeDtypeStruct((ind, columns), b...  3.44 us

profile of v3, /device:TPU:0, one launch (start us, length us, event | category | flops | bytes accessed | tf_op | source)
XLA Modules:
  0.0 94.2 jit_solution(4785469711747308705)
XLA Ops:
  0.6 89.9 %shard_map.68 = (bf16[8192,512]{1,0:T(8,128)(2,1)S(1)}, bf16[512,256]{1,0:T(8,128)(2,1)S(1)}) custom-call(bf16[64,8192]{1,0:T(8,128)(2,1)} %bitcast.3, bf16[8192,256]{1,0:T(8,128)(2,1)} %pheno.1, f32[128,128]{1,0:T(8,128)} %basis_in.1, f32[4,128]{1,0:T(4,128)} %bitcast.4, f32[1,128]{1,0:T(1,128)} %bitcast.5), custom_call_target="tpu_custom_call" | custom-call | tf_op jit(solution)/shard_map/pallas_call | solution.py:473
  90.6 3.4 %shard_map.69 = (bf16[8192,256]{1,0:T(8,128)(2,1)}, f32[128,256]{1,0:T(8,128)}) custom-call(bf16[8192,512]{1,0:T(8,128)(2,1)S(1)} %get-tuple-element.6.w, bf16[512,256]{1,0:T(8,128)(2,1)S(1)} %get-tuple-element.7.c), custom_call_target="tpu_custom_call" | custom-call | tf_op jit(solution)/shard_map/pallas_call | solution.py:504

commit v4 on v3

--- a/solution.py
+++ b/solution.py
@@ -64,18 +64,32 @@
     for copy in small:
         copy.start()
 
-    barrier = pltpu.get_barrier_semaphore()
-    for d in range(1, cols):
-        pl.semaphore_signal(barrier, inc=1, device_id=(me_r, lax.rem(me_c + d, cols)), device_id_type=MESH)
-    for d in range(1, rows):
-        pl.semaphore_signal(barrier, inc=1, device_id=(lax.rem(me_r + d, rows), me_c), device_id_type=MESH)
-    pl.semaphore_wait(barrier, cols + rows - 2)
-
     far = z // (lines // 2)
     place_of = lambda k: k + far * (lines - 1 - 2 * k)
     is_end = z == place_of(0)
     is_mid = jnp.logical_not(is_end)
     own = lambda k: 2 * place_of(k) + y
+
+    barrier = pltpu.get_barrier_semaphore()
+
+    def greet(r, c):
+        pl.semaphore_signal(barrier, inc=1, device_id=(r, c), device_id_type=MESH)
+
+    for d in range(1, rows):
+        greet(lax.rem(me_r + d, rows), me_c)
+    greet(me_r, me_c + 1 - 2 * y)
+
+    @pl.when(is_end)
+    def _():
+        greet(me_r, own(1))
+        pl.semaphore_wait(barrier, rows + 1)
+
+    @pl.when(is_mid)
+    def _():
+        greet(me_r, own(0))
+        greet(me_r, own(2))
+        pl.semaphore_wait(barrier, rows + 2)
+
     across = lambda k: 2 * place_of(k) + 1 - y
     SAME, OTHER = own, across
 
@@ -271,11 +285,12 @@
         finish_pair(1)
         first = [j for j in range(PIECES) if j not in FROM_END]
         b = len(LATE)
-        order = [(0, first[0]), (2, first[0])] + [(0, j) for j in first[1:]]
-        for i, (k, j) in enumerate(order):
+        early_y = EARLY[: n // 2]
+        for i, (k, j) in enumerate([(0, first[0]), (2, first[0]), (0, LATE[0]), (3, early_y[0])]):
             arrived(SAME, 3, b + i)
             send(0, SAME, 3, b + i)
-            send("y", SAME, 3, b + i)
+            if b + i in early_y:
+                send("y", SAME, 3, b + i)
             arrived(OTHER, k, j)
             process(k, j)
         for j in EARLY[n // 2:]:
@@ -283,16 +298,20 @@
         lent_here(0)
         for k in (0, 1):
             process_lent(k, LATE[0])
-        for i, (k, j) in enumerate([(2, j) for j in LATE] + [(3, j) for j in LATE]):
+        here = [(2, j) for j in LATE] + [(3, j) for j in LATE]
+        for (k, j), (m, i) in zip(here, [(0, LATE[1]), (3, early_y[1]), (3, early_y[2]), (2, LATE[0])]):
             arrived(SAME, k, j)
             send("y", SAME, k, j)
-            arrived(OTHER, 3, i)
-            process(3, i)
+            arrived(OTHER, m, i)
+            process(m, i)
+        for j in EARLY[n // 2:]:
+            send("y", SAME, 3, j)
         lent_here(1)
         for k in (0, 1):
             process_lent(k, LATE[1])
             finish_pair(k, 1)
-        rest = [(3, j) for j in EARLY[2 * b:]] + [(2, j) for j in LATE] + [(3, j) for j in LATE]
+        process_lent(2, LATE[0])
+        rest = [(2, LATE[1]), (3, LATE[0]), (3, LATE[1])] + [(3, j) for j in EARLY[n // 2:]]
         for i, j in enumerate(FROM_END):
             arrived(OTHER, 0, j)
             process(0, j)
@@ -303,17 +322,16 @@
             process(k, m)
             if m in LATE:
                 process_lent(k, m)
+            if m == LATE[1]:
+                finish_pair(k, 1)
             if i == MID_FEED:
                 late_steps("mid", 0)
         finish_pair(0)
         finish_pair(2)
-        finish_pair(2, 1)
         for k, m in rest:
             arrived(OTHER, k, m)
             process(k, m)
-            process_lent(k, m)
         finish_pair(3)
-        finish_pair(3, 1)
 
     def exchange_time(i):
         @pl.when(is_end)

time: 94.3 us -> 92.8 us (0.984)
  Pallas kernels: 93.4 us -> 91.9 us
    pallas_call x1, Pallas kernels: 89.9 us -> 88.4 us  [fused(): pl.pallas_call(functools.partial(gather_rotate, rows, cols), out_shape=(p...]
where the time goes in v4:
time: 92.8 us; the launch traced here: 92.7 us
  Pallas kernels  91.9 us (99%)
    pallas_call x1, Pallas kernels, fused(): pl.pallas_call(functools.partial(gather_rotate, rows, cols), out_shape=(p...  88.4 us
    pallas_call x1, Pallas kernels, fused(): pl.pallas_call(predict, out_shape=(jax.ShapeDtypeStruct((ind, columns), b...  3.44 us

profile of v4, /device:TPU:0, one launch (start us, length us, event | category | flops | bytes accessed | tf_op | source)
XLA Modules:
  0.0 92.7 jit_solution(18349115092498297442)
XLA Ops:
  0.6 88.4 %shard_map.68 = (bf16[8192,512]{1,0:T(8,128)(2,1)S(1)}, bf16[512,256]{1,0:T(8,128)(2,1)S(1)}) custom-call(bf16[64,8192]{1,0:T(8,128)(2,1)} %bitcast.3, bf16[8192,256]{1,0:T(8,128)(2,1)} %pheno.1, f32[128,128]{1,0:T(8,128)} %basis_in.1, f32[4,128]{1,0:T(4,128)} %bitcast.4, f32[1,128]{1,0:T(1,128)} %bitcast.5), custom_call_target="tpu_custom_call" | custom-call | tf_op jit(solution)/shard_map/pallas_call | solution.py:491
  89.1 3.4 %shard_map.69 = (bf16[8192,256]{1,0:T(8,128)(2,1)}, f32[128,256]{1,0:T(8,128)}) custom-call(bf16[8192,512]{1,0:T(8,128)(2,1)S(1)} %get-tuple-element.6.w, bf16[512,256]{1,0:T(8,128)(2,1)S(1)} %get-tuple-element.7.c), custom_call_target="tpu_custom_call" | custom-call | tf_op jit(solution)/shard_map/pallas_call | solution.py:522

commit v5 on v4

--- a/solution.py
+++ b/solution.py
@@ -31,13 +31,14 @@
     (),
 )
 TILES = 16
+AHEAD = 8
 MESH = pl.DeviceIdType.MESH
 HIGH = lax.Precision.HIGHEST
 
 
 def gather_rotate(
     rows, cols, q, pheno, basis_in, kin_in, trait_in,
-    w_out, c_out,
+    w_out, c_out, held,
     basis, kin, trait, g, ph, lent, acc, lent_acc, part_f, part, rparts, sb, rb, ob, crow, ct,
     load_sem, bulk_send, recv_sem, lend_recv, small_send, rs_recv, trade_recv, ag_recv,
 ):
@@ -99,7 +100,7 @@
 
     def sends_done(counts):
         for i, count in enumerate(counts):
-            rows_of = w_out.at[pl.ds(0, count * width * piece // w_out.shape[1])]
+            rows_of = w_out.at[pl.ds(0, int(count * width * piece) // w_out.shape[1])]
             pltpu.make_async_copy(rows_of, rows_of, bulk_send.at[i]).wait()
 
     def hop(way, kind, k, j):
@@ -435,6 +436,9 @@
     for p in row_peers:
         share(p, p).wait_recv()
         place(p)
+    size = people // TILES
+    for i in range(held.shape[0] // size):
+        held[i * size:(i + 1) * size, :] = tile_of(w_out, c_out, i * size, size)
     exchange_time(5)
 
     def count(sent, others, late):
@@ -447,11 +451,11 @@
 
     @pl.when(is_end)
     def _():
-        sends_done([int(c) for c in count(end_sent, PIECES, len(late_sent["end"]))])
+        sends_done(count(end_sent, PIECES, len(late_sent["end"])))
 
     @pl.when(is_mid)
     def _():
-        sends_done([int(c) for c in count(mid_sent, 0, len(late_sent["mid"]))])
+        sends_done(count(mid_sent, 0, len(late_sent["mid"])))
         all_but_one(part.at[1], small_send.at[1])
 
     all_but_one(part.at[0], small_send.at[0])
@@ -460,18 +464,26 @@
     all_but_one(crow, small_send.at[4])
 
 
-def predict(w, c, gen_out, coeffs_out, held, coeffs, gen_sem):
+def tile_of(w, c, first, size):
+    return jnp.dot(w[first:first + size, :], c[...], preferred_element_type=jnp.float32).astype(jnp.bfloat16)
+
+
+def predict(w, c, ready, gen_out, coeffs_out, held, coeffs, gen_sem):
     share = coeffs.shape[0]
     size = w.shape[0] // TILES
-    mine = pl.ds(pl.multiple_of(lax.axis_index("row") * share, share), share)
-    coeffs[...] = c[mine, :].astype(jnp.float32)
-    copies = [pltpu.make_async_copy(coeffs, coeffs_out, gen_sem.at[TILES])]
+    done = ready.shape[0]
+    copies = [pltpu.make_async_copy(ready, gen_out.at[pl.ds(0, done)], gen_sem.at[0])]
     copies[0].start()
-    for i in range(TILES):
+    for i in range(done // size, TILES):
         at = pl.ds(i * size, size)
-        held[at, :] = jnp.dot(w[at, :], c[...], preferred_element_type=jnp.float32).astype(jnp.bfloat16)
+        held[at, :] = tile_of(w, c, i * size, size)
         copies.append(pltpu.make_async_copy(held.at[at], gen_out.at[at], gen_sem.at[i]))
         copies[-1].start()
+        if i == done // size:
+            mine = pl.ds(pl.multiple_of(lax.axis_index("row") * share, share), share)
+            coeffs[...] = c[mine, :].astype(jnp.float32)
+            copies.append(pltpu.make_async_copy(coeffs, coeffs_out, gen_sem.at[TILES]))
+            copies[-1].start()
     for copy in copies:
         copy.wait()
 
@@ -488,14 +500,15 @@
     lot = columns // cols
     dma = pltpu.SemaphoreType.DMA
     given = (panel.T, pheno, trait_basis, kin_values.reshape(rows, share), trait_values[None, :])
-    whole, low = pl.pallas_call(
+    whole, low, ready = pl.pallas_call(
         functools.partial(gather_rotate, rows, cols),
         out_shape=(
             pltpu.VMEM((ind, rows * share), bf),
             pltpu.VMEM((rows * share, columns), bf),
+            pltpu.VMEM((ind * AHEAD // TILES, columns), bf),
         ),
         in_specs=[hbm] * 5,
-        out_specs=(vmem, vmem),
+        out_specs=(vmem, vmem, vmem),
         scratch_shapes=[
             pltpu.VMEM((traits, traits), f32),
             pltpu.VMEM((rows, share), f32),
@@ -525,11 +538,11 @@
             jax.ShapeDtypeStruct((ind, columns), bf),
             jax.ShapeDtypeStruct((share, columns), f32),
         ),
-        in_specs=[vmem] * 2,
+        in_specs=[vmem] * 3,
         out_specs=(hbm, hbm),
         scratch_shapes=[pltpu.VMEM((ind, columns), bf), pltpu.VMEM((share, columns), f32), dma((TILES + 1,))],
         compiler_params=pltpu.CompilerParams(vmem_limit_bytes=20 * 1024 * 1024),
-    )(whole, low)
+    )(whole, low, ready)
     return coeffs, genetic
 
 

time: 92.8 us -> 91.8 us (0.989)
  Pallas kernels: 91.9 us -> 90.7 us
    pallas_call x1, Pallas kernels: 3.44 us -> 2.26 us  [fused(): pl.pallas_call(predict, out_shape=(jax.ShapeDtypeStruct((ind, columns), b...]
where the time goes in v5:
time: 91.8 us; the launch traced here: 91.5 us
  Pallas kernels  90.7 us (99%)
    pallas_call x1, Pallas kernels, fused(): pl.pallas_call(functools.partial(gather_rotate, rows, cols), out_shape=(p...  88.4 us
    pallas_call x1, Pallas kernels, fused(): pl.pallas_call(predict, out_shape=(jax.ShapeDtypeStruct((ind, columns), b...  2.26 us

profile of v5, /device:TPU:0, one launch (start us, length us, event | category | flops | bytes accessed | tf_op | source)
XLA Modules:
  0.0 91.5 jit_solution(5710800273177711391)
XLA Ops:
  0.6 88.4 %shard_map.68 = (bf16[8192,512]{1,0:T(8,128)(2,1)S(1)}, bf16[512,256]{1,0:T(8,128)(2,1)S(1)}, bf16[4096,256]{1,0:T(8,128)(2,1)S(1)}) custom-call(bf16[64,8192]{1,0:T(8,128)(2,1)} %bitcast.3, bf16[8192,256]{1,0:T(8,128)(2,1)} %pheno.1, f32[128,128]{1,0:T(8,128)} %basis_in.1, f32[4,128]{1,0:T(4,128)} %bitcast.4, f32[1,128]{1,0:T(1,128)} %bitcast.5), custom_call_target="tpu_custom_call" | custom-call | tf_op jit(solution)/shard_map/pallas_call | solution.py:503
  89.1 2.3 %shard_map.69 = (bf16[8192,256]{1,0:T(8,128)(2,1)}, f32[128,256]{1,0:T(8,128)}) custom-call(bf16[8192,512]{1,0:T(8,128)(2,1)S(1)} %get-tuple-element.7.w, bf16[512,256]{1,0:T(8,128)(2,1)S(1)} %get-tuple-element.8.c, bf16[4096,256]{1,0:T(8,128)(2,1)S(1)} %get-tuple-element.9.ready), custom_call_target="tpu_custom_call" | custom-call | tf_op jit(solution)/shard_map/pallas_call | solution.py:535

commit v6 on v5

--- a/solution.py
+++ b/solution.py
@@ -17,10 +17,10 @@
 END_STEPS = (
     ("P10", "P11"),
     ("P20", "T00", "P21", "T01"),
-    ("P22", "T02"),
-    ("T03", "P23", "P30", "T10", "T11", "P31", "T20"),
-    ("P32", "P33", "T21", "T22", "T23"),
-    ("T30", "T31", "T32", "T33", "B12", "B13"),
+    ("P22", "T02", "P23"),
+    ("P30", "T03", "P31", "P32", "T10", "T11", "T20"),
+    ("P33", "T21", "T22", "T23", "T30", "T31"),
+    ("T32", "T33", "B12", "B13"),
 )
 MID_STEPS = (
     ("O10", "O11", "O20", "O21", "O22"),
@@ -355,7 +355,7 @@
         part_f[...] = total.T
         by_set = [part_f[pl.ds(s, t_here, stride=sets), :] for s in range(sets)]
         turned = jnp.concatenate(by_set, axis=0).astype(jnp.bfloat16)
-        sb[:, h] = turned.reshape(cols, columns // cols, LANES)
+        sb[h] = turned.reshape(cols, columns // cols, LANES)
 
     total_of(0)
 
@@ -363,13 +363,10 @@
     def _():
         total_of(1)
 
-    @pl.when(is_end)
-    def _():
-        sb[:, 1] = jnp.zeros_like(sb[:, 1])
-
-    def trade1(peer, slot):
+    def trade1(peer, slot, h):
         return pltpu.make_async_remote_copy(
-            src_ref=sb.at[peer], dst_ref=rb.at[slot], send_sem=small_send.at[2], recv_sem=trade_recv.at[0],
+            src_ref=sb.at[h, peer], dst_ref=rb.at[h, slot],
+            send_sem=small_send.at[(2, 5)[h]], recv_sem=trade_recv.at[(0, 2)[h]],
             device_id=(me_r, peer), device_id_type=MESH,
         )
 
@@ -388,24 +385,38 @@
     col_peers = [lax.rem(me_c + d, cols) for d in range(1, cols)]
     row_peers = [lax.rem(me_r + d, rows) for d in range(1, rows)]
     for p in col_peers:
-        trade1(p, me_c).start()
+        trade1(p, me_c, 0).start()
+
+    @pl.when(is_mid)
+    def _():
+        for p in col_peers:
+            trade1(p, me_c, 1).start()
+        rb[1, me_c] = sb[1, me_c]
+
     exchange_time(1)
     exchange_time(2)
-    rb[me_c] = sb[me_c]
+    rb[0, me_c] = sb[0, me_c]
     for copy in small:
         copy.wait()
     product = kin[pl.ds(me_r, 1), :] * jnp.broadcast_to(trait[...], (LANES, traits)).T
     weight = product / (product + 1.0)
-    all_but_one(rb, trade_recv.at[0])
+    all_but_one(rb.at[0], trade_recv.at[0])
+    for role, senders in ((is_end, cols - 4), (is_mid, cols - 5)):
+
+        @pl.when(role)
+        def _():
+            some = rb.at[1, pl.ds(0, senders)]
+            pltpu.make_async_copy(some, some, trade_recv.at[2]).wait()
+
     s_here = sets // cols
 
     def gathered(s):
         at = slice(s * t_here, (s + 1) * t_here)
         terms = []
         for c in range(cols):
-            term = rb[c, 0, at, :].astype(jnp.float32)
+            term = rb[0, c, at, :].astype(jnp.float32)
             if c // 2 in (0, lines - 1):
-                term = term + rb[c + 2 if c // 2 == 0 else c - 2, 1, at, :].astype(jnp.float32)
+                term = term + rb[1, c + 2 if c // 2 == 0 else c - 2, at, :].astype(jnp.float32)
             terms.append(term)
         return jnp.concatenate(terms, axis=0)
 
@@ -457,9 +468,10 @@
     def _():
         sends_done(count(mid_sent, 0, len(late_sent["mid"])))
         all_but_one(part.at[1], small_send.at[1])
+        all_but_one(sb.at[1], small_send.at[5])
 
     all_but_one(part.at[0], small_send.at[0])
-    all_but_one(sb, small_send.at[2])
+    all_but_one(sb.at[0], small_send.at[2])
     all_but_one(ob, small_send.at[3])
     all_but_one(crow, small_send.at[4])
 
@@ -521,12 +533,12 @@
             pltpu.VMEM((columns, LANES), f32),
             pltpu.VMEM((2, rows, share, columns), bf),
             pltpu.VMEM((2, rows, share, columns), bf),
-            pltpu.VMEM((cols, 2, lot, LANES), bf),
-            pltpu.VMEM((cols, 2, lot, LANES), bf),
+            pltpu.VMEM((2, cols, lot, LANES), bf),
+            pltpu.VMEM((2, cols, lot, LANES), bf),
             pltpu.VMEM((cols, lot, LANES), bf),
             pltpu.VMEM((rows, cols, lot, LANES), bf),
             pltpu.VMEM((columns, LANES), f32),
-            dma((5,)), dma((2,)), dma((cols, len(EARLY) + UNITS)), dma((len(LATE),)), dma((5,)), dma((2,)), dma((2,)), dma((rows,)),
+            dma((5,)), dma((2,)), dma((cols, len(EARLY) + UNITS)), dma((len(LATE),)), dma((6,)), dma((2,)), dma((3,)), dma((rows,)),
         ],
         compiler_params=pltpu.CompilerParams(
             collective_id=0, has_side_effects=True, vmem_limit_bytes=36 * 1024 * 1024

time: 91.8 us -> 91.6 us (level)
  no operation moved by 1% of the time
where the time goes in v6:
time: 91.6 us; the launch traced here: 91.2 us
  Pallas kernels  90.4 us (99%)
    pallas_call x1, Pallas kernels, fused(): pl.pallas_call(functools.partial(gather_rotate, rows, cols), out_shape=(p...  88.1 us
    pallas_call x1, Pallas kernels, fused(): pl.pallas_call(predict, out_shape=(jax.ShapeDtypeStruct((ind, columns), b...  2.26 us

profile of v6, /device:TPU:0, one launch (start us, length us, event | category | flops | bytes accessed | tf_op | source)
XLA Modules:
  0.0 91.2 jit_solution(15583977235164609712)
XLA Ops:
  0.6 88.1 %shard_map.68 = (bf16[8192,512]{1,0:T(8,128)(2,1)S(1)}, bf16[512,256]{1,0:T(8,128)(2,1)S(1)}, bf16[4096,256]{1,0:T(8,128)(2,1)S(1)}) custom-call(bf16[64,8192]{1,0:T(8,128)(2,1)} %bitcast.3, bf16[8192,256]{1,0:T(8,128)(2,1)} %pheno.1, f32[128,128]{1,0:T(8,128)} %basis_in.1, f32[4,128]{1,0:T(4,128)} %bitcast.4, f32[1,128]{1,0:T(1,128)} %bitcast.5), custom_call_target="tpu_custom_call" | custom-call | tf_op jit(solution)/shard_map/pallas_call | solution.py:515
  88.7 2.3 %shard_map.69 = (bf16[8192,256]{1,0:T(8,128)(2,1)}, f32[128,256]{1,0:T(8,128)}) custom-call(bf16[8192,512]{1,0:T(8,128)(2,1)S(1)} %get-tuple-element.7.w, bf16[512,256]{1,0:T(8,128)(2,1)S(1)} %get-tuple-element.8.c, bf16[4096,256]{1,0:T(8,128)(2,1)S(1)} %get-tuple-element.9.ready), custom_call_target="tpu_custom_call" | custom-call | tf_op jit(solution)/shard_map/pallas_call | solution.py:547

commit v7 on v6

--- a/solution.py
+++ b/solution.py
@@ -355,7 +355,7 @@
         part_f[...] = total.T
         by_set = [part_f[pl.ds(s, t_here, stride=sets), :] for s in range(sets)]
         turned = jnp.concatenate(by_set, axis=0).astype(jnp.bfloat16)
-        sb[h] = turned.reshape(cols, columns // cols, LANES)
+        sb[h] = turned.reshape(sb.shape[1:])
 
     total_of(0)
 
@@ -365,14 +365,14 @@
 
     def trade1(peer, slot, h):
         return pltpu.make_async_remote_copy(
-            src_ref=sb.at[h, peer], dst_ref=rb.at[h, slot],
+            src_ref=sb.at[h, peer - 2], dst_ref=rb.at[h, slot],
             send_sem=small_send.at[(2, 5)[h]], recv_sem=trade_recv.at[(0, 2)[h]],
             device_id=(me_r, peer), device_id_type=MESH,
         )
 
     def trade2(peer, slot):
         return pltpu.make_async_remote_copy(
-            src_ref=ob.at[peer], dst_ref=crow.at[me_r, slot], send_sem=small_send.at[3], recv_sem=trade_recv.at[1],
+            src_ref=ob.at[peer], dst_ref=crow.at[me_r, slot - 2], send_sem=small_send.at[3], recv_sem=trade_recv.at[1],
             device_id=(me_r, peer), device_id_type=MESH,
         )
 
@@ -384,31 +384,23 @@
 
     col_peers = [lax.rem(me_c + d, cols) for d in range(1, cols)]
     row_peers = [lax.rem(me_r + d, rows) for d in range(1, rows)]
-    for p in col_peers:
-        trade1(p, me_c, 0).start()
-
-    @pl.when(is_mid)
-    def _():
-        for p in col_peers:
-            trade1(p, me_c, 1).start()
-        rb[1, me_c] = sb[1, me_c]
+    for p in range(2, cols - 2):
+
+        @pl.when(p != me_c)
+        def _():
+            trade1(p, me_c, 0).start()
+
+            @pl.when(is_mid)
+            def _():
+                trade1(p, me_c, 1).start()
 
     exchange_time(1)
     exchange_time(2)
-    rb[0, me_c] = sb[0, me_c]
     for copy in small:
         copy.wait()
     product = kin[pl.ds(me_r, 1), :] * jnp.broadcast_to(trait[...], (LANES, traits)).T
     weight = product / (product + 1.0)
-    all_but_one(rb.at[0], trade_recv.at[0])
-    for role, senders in ((is_end, cols - 4), (is_mid, cols - 5)):
-
-        @pl.when(role)
-        def _():
-            some = rb.at[1, pl.ds(0, senders)]
-            pltpu.make_async_copy(some, some, trade_recv.at[2]).wait()
-
-    s_here = sets // cols
+    s_here = sets // (cols - 4)
 
     def gathered(s):
         at = slice(s * t_here, (s + 1) * t_here)
@@ -420,19 +412,35 @@
             terms.append(term)
         return jnp.concatenate(terms, axis=0)
 
-    got = jnp.concatenate([gathered(s) for s in range(s_here)], axis=1)
-    rotated = jnp.dot(basis[...].T, got, precision=HIGH, preferred_element_type=jnp.float32)
-    scaled = rotated * jnp.concatenate([weight] * s_here, axis=1)
-    back = jnp.dot(basis[...], scaled, precision=HIGH, preferred_element_type=jnp.float32)
-    for s in range(s_here):
-        ob[:, s * t_here:(s + 1) * t_here, :] = (
-            back[:, s * LANES:(s + 1) * LANES].reshape(cols, t_here, LANES).astype(jnp.bfloat16)
-        )
-    for p in col_peers:
-        trade2(p, me_c).start()
+    @pl.when(is_mid)
+    def _():
+        for h in range(2):
+            rb[h, me_c] = sb[h, me_c - 2]
+        all_but_one(rb.at[0], trade_recv.at[0])
+        some = rb.at[1, pl.ds(0, cols - 5)]
+        pltpu.make_async_copy(some, some, trade_recv.at[2]).wait()
+        got = jnp.concatenate([gathered(s) for s in range(s_here)], axis=1)
+        rotated = jnp.dot(basis[...].T, got, precision=HIGH, preferred_element_type=jnp.float32)
+        scaled = rotated * jnp.concatenate([weight] * s_here, axis=1)
+        back = jnp.dot(basis[...], scaled, precision=HIGH, preferred_element_type=jnp.float32)
+        for s in range(s_here):
+            ob[:, s * t_here:(s + 1) * t_here, :] = (
+                back[:, s * LANES:(s + 1) * LANES].reshape(cols, t_here, LANES).astype(jnp.bfloat16)
+            )
+        for p in col_peers:
+            trade2(p, me_c).start()
+        crow[me_r, me_c - 2] = ob[me_c]
+
     exchange_time(3)
-    crow[me_r, me_c] = ob[me_c]
-    all_but_one(ob, trade_recv.at[1])
+    def blocks_done(ref, sem, when_end, when_mid):
+        for role, amount in ((is_end, when_end), (is_mid, when_mid)):
+
+            @pl.when(role)
+            def _():
+                some = ref.at[pl.ds(0, amount)]
+                pltpu.make_async_copy(some, some, sem).wait()
+
+    blocks_done(ob, trade_recv.at[1], cols - 4, cols - 5)
     for p in row_peers:
         share(p, me_r).start()
 
@@ -469,10 +477,10 @@
         sends_done(count(mid_sent, 0, len(late_sent["mid"])))
         all_but_one(part.at[1], small_send.at[1])
         all_but_one(sb.at[1], small_send.at[5])
+        all_but_one(ob, small_send.at[3])
 
     all_but_one(part.at[0], small_send.at[0])
-    all_but_one(sb.at[0], small_send.at[2])
-    all_but_one(ob, small_send.at[3])
+    blocks_done(sb.at[0], small_send.at[2], cols - 4, cols - 5)
     all_but_one(crow, small_send.at[4])
 
 
@@ -509,7 +517,6 @@
     bf, f32 = jnp.bfloat16, jnp.float32
     hbm = pl.BlockSpec(memory_space=pltpu.HBM)
     vmem = pl.BlockSpec(memory_space=pltpu.VMEM)
-    lot = columns // cols
     dma = pltpu.SemaphoreType.DMA
     given = (panel.T, pheno, trait_basis, kin_values.reshape(rows, share), trait_values[None, :])
     whole, low, ready = pl.pallas_call(
@@ -533,10 +540,10 @@
             pltpu.VMEM((columns, LANES), f32),
             pltpu.VMEM((2, rows, share, columns), bf),
             pltpu.VMEM((2, rows, share, columns), bf),
-            pltpu.VMEM((2, cols, lot, LANES), bf),
-            pltpu.VMEM((2, cols, lot, LANES), bf),
-            pltpu.VMEM((cols, lot, LANES), bf),
-            pltpu.VMEM((rows, cols, lot, LANES), bf),
+            pltpu.VMEM((2, cols - 4, columns // (cols - 4), LANES), bf),
+            pltpu.VMEM((2, cols, columns // (cols - 4), LANES), bf),
+            pltpu.VMEM((cols, columns // (cols - 4), LANES), bf),
+            pltpu.VMEM((rows, cols - 4, columns // (cols - 4), LANES), bf),
             pltpu.VMEM((columns, LANES), f32),
             dma((5,)), dma((2,)), dma((cols, len(EARLY) + UNITS)), dma((len(LATE),)), dma((6,)), dma((2,)), dma((3,)), dma((rows,)),
         ],

time: 91.6 us -> 90.8 us (level)
  Pallas kernels: 90.4 us -> 89.2 us
    pallas_call x1, Pallas kernels: 88.1 us -> 87 us  [fused(): pl.pallas_call(functools.partial(gather_rotate, rows, cols), out_shape=(p...]
where the time goes in v7:
time: 90.8 us; the launch traced here: 90 us
  Pallas kernels  89.2 us (98%)
    pallas_call x1, Pallas kernels, fused(): pl.pallas_call(functools.partial(gather_rotate, rows, cols), out_shape=(p...  87 us
    pallas_call x1, Pallas kernels, fused(): pl.pallas_call(predict, out_shape=(jax.ShapeDtypeStruct((ind, columns), b...  2.26 us

profile of v7, /device:TPU:0, one launch (start us, length us, event | category | flops | bytes accessed | tf_op | source)
XLA Modules:
  0.0 90.0 jit_solution(11399711936496245724)
XLA Ops:
  0.6 87.0 %shard_map.68 = (bf16[8192,512]{1,0:T(8,128)(2,1)S(1)}, bf16[512,256]{1,0:T(8,128)(2,1)S(1)}, bf16[4096,256]{1,0:T(8,128)(2,1)S(1)}) custom-call(bf16[64,8192]{1,0:T(8,128)(2,1)} %bitcast.3, bf16[8192,256]{1,0:T(8,128)(2,1)} %pheno.1, f32[128,128]{1,0:T(8,128)} %basis_in.1, f32[4,128]{1,0:T(4,128)} %bitcast.4, f32[1,128]{1,0:T(1,128)} %bitcast.5), custom_call_target="tpu_custom_call" | custom-call | tf_op jit(solution)/shard_map/pallas_call | solution.py:522
  87.6 2.3 %shard_map.69 = (bf16[8192,256]{1,0:T(8,128)(2,1)}, f32[128,256]{1,0:T(8,128)}) custom-call(bf16[8192,512]{1,0:T(8,128)(2,1)S(1)} %get-tuple-element.7.w, bf16[512,256]{1,0:T(8,128)(2,1)S(1)} %get-tuple-element.8.c, bf16[4096,256]{1,0:T(8,128)(2,1)S(1)} %get-tuple-element.9.ready), custom_call_target="tpu_custom_call" | custom-call | tf_op jit(solution)/shard_map/pallas_call | solution.py:554

commit v8 on v7

--- a/solution.py
+++ b/solution.py
@@ -31,7 +31,7 @@
     (),
 )
 TILES = 16
-AHEAD = 8
+AHEAD = 7
 MESH = pl.DeviceIdType.MESH
 HIGH = lax.Precision.HIGHEST
 

time: 90.8 us -> 90.8 us (level)
  no operation moved by 1% of the time
where the time goes in v8:
time: 90.8 us; the launch traced here: 90 us
  Pallas kernels  89.2 us (98%)
    pallas_call x1, Pallas kernels, fused(): pl.pallas_call(functools.partial(gather_rotate, rows, cols), out_shape=(p...  86.8 us
    pallas_call x1, Pallas kernels, fused(): pl.pallas_call(predict, out_shape=(jax.ShapeDtypeStruct((ind, columns), b...  2.4 us

profile of v8, /device:TPU:0, one launch (start us, length us, event | category | flops | bytes accessed | tf_op | source)
XLA Modules:
  0.0 90.0 jit_solution(3509246691643990526)
XLA Ops:
  0.6 86.8 %shard_map.68 = (bf16[8192,512]{1,0:T(8,128)(2,1)S(1)}, bf16[512,256]{1,0:T(8,128)(2,1)S(1)}, bf16[3584,256]{1,0:T(8,128)(2,1)S(1)}) custom-call(bf16[64,8192]{1,0:T(8,128)(2,1)} %bitcast.3, bf16[8192,256]{1,0:T(8,128)(2,1)} %pheno.1, f32[128,128]{1,0:T(8,128)} %basis_in.1, f32[4,128]{1,0:T(4,128)} %bitcast.4, f32[1,128]{1,0:T(1,128)} %bitcast.5), custom_call_target="tpu_custom_call" | custom-call | tf_op jit(solution)/shard_map/pallas_call | solution.py:522
  87.5 2.4 %shard_map.69 = (bf16[8192,256]{1,0:T(8,128)(2,1)}, f32[128,256]{1,0:T(8,128)}) custom-call(bf16[8192,512]{1,0:T(8,128)(2,1)S(1)} %get-tuple-element.7.w, bf16[512,256]{1,0:T(8,128)(2,1)S(1)} %get-tuple-element.8.c, bf16[3584,256]{1,0:T(8,128)(2,1)S(1)} %get-tuple-element.9.ready), custom_call_target="tpu_custom_call" | custom-call | tf_op jit(solution)/shard_map/pallas_call | solution.py:554
